TPU v7x, 32 devices: a whole 2x2x4 slice. The times are simulated.
32 devices in a mesh: band: 8 (over z, x), coef: 4 (over y, core).
Axes of the slice: x: 2, y: 2, z: 4, core: 2. Of those that a mesh axis runs over, the one named last changes fastest.
Arguments:
- coeffs: float32 [1024, 262144], P('band', 'coef'), may hold values from -320 to 320
- ref_block: float32 [1024, 262144], P('band', 'coef'), may hold values from -0.01171875 to 0.01171875
- index_map: int32 [262144], P('coef'), may hold values from 0 to 65535, as said below
- band_group: int32 [1024], P('band'), may hold values from 0 to 15
Outputs:
- ortho: float32 [1024, 262144], P('band', 'coef')
- band_residual: float32 [1024], P('band')
- group_residual: float32 [16], replicated
Inputs may be any that keep to these rules, and one draw needn't show every extreme that they name: Within each aligned slab of 65536 coefficients, index_map holds every number of 0 to 65535 once.
All inputs are finite; a program needn't handle non-finite values.
Results may differ from a plain program's by a relative error of at most 0.000098.
Values sent between devices are 32-bit elements; how exact they have to be, the bound alone decides.
No kernel may reach another device: no remote copies, remote signals or barrier semaphores. Data moves between devices by JAX's collectives and lax.ppermute only.
A program may use at most 384 MiB of HBM per device.

v0:
```python
import jax
import jax.numpy as jnp
from jax import lax
from jax.sharding import PartitionSpec as P

NB = 1024
NGROUPS = 16


def local(coeffs, ref_block, index_map, band_group):
    columns = lax.all_to_all(coeffs, "band", split_axis=1, concat_axis=0, tiled=True)
    partial_value = jnp.dot(
        columns, columns.T, precision=lax.Precision.HIGHEST, preferred_element_type=jnp.float32
    )
    margin = lax.psum(partial_value, ("band", "coef"))
    factor = jnp.linalg.cholesky(margin)
    ortho_cols = lax.linalg.triangular_solve(factor, columns, left_side=True, lower=True)
    ortho = lax.all_to_all(ortho_cols, "band", split_axis=0, concat_axis=1, tiled=True)
    aligned = jnp.take(ortho, index_map, axis=1)
    squares = jnp.sum((aligned - ref_block) ** 2, axis=1)
    group_range = jnp.arange(NGROUPS, dtype=jnp.int32)
    totals = lax.psum(squares, "coef")
    band_residual = jnp.sqrt(totals + 1e-06)
    onehot = (band_group[:, None] == group_range[None, :]).astype(jnp.float32)
    terms = jnp.dot(
        band_residual, onehot, precision=lax.Precision.HIGHEST, preferred_element_type=jnp.float32
    )
    group_residual = lax.psum(terms, "band") * (NGROUPS / NB)
    return (ortho, band_residual, group_residual)


def solution(mesh):
    return jax.shard_map(
        local,
        mesh=mesh,
        in_specs=(P("band", "coef"), P("band", "coef"), P("coef"), P("band")),
        out_specs=(P("band", "coef"), P("band"), P()),
        check_vma=False,
    )
```

profile of v0, /device:TPU:0, one launch (start us, length us, event | category | flops | bytes accessed | tf_op | source)
XLA Modules:
  0.0 2639.5 jit_solution(11342121475017291769)
XLA Ops:
  7.2 33.4 %copy.17 = f32[128,65536]{0,1:T(8,128)} copy(f32[128,65536]{1,0:T(8,128)} %param.4) | data formatting | bytes 67108864 | tf_op args[0]
  40.6 31.1 %copy.18 = f32[128,8,8192]{2,0,1:T(8,128)} copy(f32[128,8,8192]{0,2,1:T(8,128)} %bitcast.156) | data formatting | bytes 67108864 | tf_op jit(solution)/shard_map/all_to_all | solution.py:11
  71.7 735.1 %all_to_all.38 = f32[128,8,8192]{2,0,1:T(8,128)} all-to-all(f32[128,8,8192]{2,0,1:T(8,128)} %copy.18), channel_id=1, replica_groups=mesh['band'=8,'coef'=4] {'band'}, dimensions={1} | all-to-all | bytes 67108864 | tf_op jit(solution)/shard_map/all_to_all | solution.py:11
  806.8 117.0 %fusion.74 = f32[1024,1024]{0,1:T(8,128)} fusion(f32[1024,8192]{1,0:T(8,128)} %bitcast.157), kind=kOutput, calls=%fused_computation.177 | convolution fusion | flops 103079215104 | bytes 37748736 | tf_op jit(solution)/shard_map/dot_general | solution.py:12
  923.9 141.6 %all-reduce.3.cloned.1.call-done = f32[1024,1024]{0,1:T(8,128)} async-done(((f32[1024,1024]{0,1:T(8,128)}), f32[1024,1024]{0,1:T(8,128)}) %all-reduce.3.cloned.1.call-update) | async-done | bytes 4194320 | tf_op jit(solution)/shard_map/psum | solution.py:15
  1065.5 5.8 copy.20
  1071.3 4.4 fusion.26
  1077.8 11.7 cholesky.223
  1089.5 9.8 custom-call.62
  1099.3 2.5 cholesky.255
  1101.9 2.3 constant_dynamic-update-slice_fusion.32
  1105.8 11.9 cholesky.244
  1118.3 9.8 custom-call.63
  1129.3 2.1 convolution_subtract_fusion.6
  1131.4 11.7 cholesky.468
  1144.4 9.8 custom-call.64
  1155.3 2.3 convolution_subtract_fusion.7
  1157.7 11.9 cholesky.487
  1170.9 9.8 custom-call.65
  1181.7 2.3 convolution_subtract_fusion.8
  1184.1 11.7 cholesky.506
  1197.1 10.2 custom-call.66
  1208.3 2.4 convolution_subtract_fusion.9
  1210.7 11.7 cholesky.526
  1223.7 9.8 custom-call.67
  1234.4 2.0 convolution_subtract_fusion.10
  1236.5 11.9 cholesky.546
  1249.7 9.8 custom-call.68
  1262.1 11.7 cholesky.564
  1280.8 4.8 select_select_fusion
  1285.6 23.2 while.1
  1286.2 2.3 bitcast_dynamic-update-slice_fusion.2
  1289.1 2.3 bitcast_dynamic-update-slice_fusion.2
  1292.0 2.3 bitcast_dynamic-update-slice_fusion.2
  1294.9 2.3 bitcast_dynamic-update-slice_fusion.2
  1297.8 2.3 bitcast_dynamic-update-slice_fusion.2
  1300.7 2.3 bitcast_dynamic-update-slice_fusion.2
  1303.6 2.3 bitcast_dynamic-update-slice_fusion.2
  1306.5 2.2 bitcast_dynamic-update-slice_fusion.2
  1308.8 78.8 %custom-call.69 = f32[8,128,128]{1,2,0:T(8,128)S(1)} custom-call(f32[8,128,128]{2,1,0:T(8,128)S(1)} %get-tuple-element.10), custom_call_target="InvertDiagBlocksLowerTriangular" | custom-call | tf_op jit(solution)/shard_map/triangular_solve | solution.py:17
  1387.6 12.6 constant_dynamic-update-slice_fusion.17
  1400.2 6.9 convolution_subtract_fusion.1
  1407.1 8.2 constant_dynamic-update-slice_fusion.16
  1415.3 7.7 convolution_subtract_fusion
  1423.0 8.6 constant_dynamic-update-slice_fusion.15
  1431.7 12.2 fusion.16
  1443.9 13.9 constant_dynamic-update-slice_fusion.14
  1457.7 14.0 fusion.19
  1471.8 12.5 constant_dynamic-update-slice_fusion.13
  1484.3 17.1 convolution_subtract_fusion.2
  1501.4 6.7 constant_dynamic-update-slice_fusion.12
  1508.1 19.2 convolution_subtract_fusion.4
  1527.3 5.8 constant_dynamic-update-slice_fusion.11
  1533.2 23.5 convolution_subtract_fusion.3
  1556.7 7.9 convolution_dynamic-update-slice_fusion
  1564.6 7.1 all-to-all-start.1
  1571.7 33.4 %copy.22 = f32[128,65536]{0,1:T(8,128)} copy(f32[128,65536]{1,0:T(8,128)} %param.5) | data formatting | bytes 67108864 | tf_op args[1]
  1605.3 687.3 %all-to-all-done.1 = f32[8,128,8192]{2,1,0:T(8,128)} async-done(((f32[8,128,8192]{2,1,0:T(8,128)}), f32[8,128,8192]{2,1,0:T(8,128)}, u32[]{:S(2)}, u32[]{:S(2)}) %all-to-all-start.1) | async-done | bytes 33554464 | tf_op jit(solution)/shard_map/all_to_all | solution.py:18
  2292.6 31.0 %copy.21 = f32[128,8,8192]{0,2,1:T(8,128)} copy(f32[128,8,8192]{2,0,1:T(8,128)} %bitcast.35) | data formatting | bytes 67108864 | tf_op jit(solution)/shard_map/all_to_all | solution.py:18
  2323.6 228.0 %gather_fusion = f32[65536,128]{1,0:T(8,128)} fusion(f32[128,65536]{0,1:T(8,128)} %bitcast.154, s32[65536]{0:T(1024)S(1)} %fusion.45), kind=kCustom, calls=%fused_computation | custom fusion | bytes 67371008 | tf_op jit(solution)/shard_map/jit(_take)/gather | solution.py:19
  2551.6 20.7 fusion.1
  2572.3 5.7 psum.22
  2578.2 33.5 %copy.23 = f32[128,65536]{1,0:T(8,128)} copy(f32[128,65536]{0,1:T(8,128)} %bitcast.155) | data formatting | bytes 67108864
  2611.6 20.3 psum.23
  (70 shorter events, 26.5 us)
Async XLA Ops:
  7.2 1058.3 %all-reduce.3.cloned.1.call-start = ((), (), s32[]{:S(2)}) async-start(), calls=%async_computation.2 | async-start | bytes 8388608 | tf_op jit(solution)/shard_map/psum | solution.py:15
  1075.7 2.0 copy-start.3
  1400.2 31.5 %copy-start = (f32[128,8192]{1,0:T(8,128)}, f32[128,8192]{1,0:T(8,128)S(1)}, u32[]{:S(2)}) copy-start(f32[128,8192]{1,0:T(8,128)S(1)} %get-tuple-element.79) | copy-start | bytes 12582916
  1415.3 16.4 copy-start.1
  1431.7 12.2 copy-start.2
  1564.6 728.0 %all-to-all-start.1 = ((f32[8,128,8192]{2,1,0:T(8,128)}), f32[8,128,8192]{2,1,0:T(8,128)}, u32[]{:S(2)}, u32[]{:S(2)}) async-start(f32[8,128,8192]{2,1,0:T(8,128)} %bitcast.166), calls=%async_computation.1 | async-start | bytes 67108864 | tf_op jit(solution)/shard_map/all_to_all | solution.py:18
  1571.7 33.4 %copy-start.4 = (s32[65536]{0:T(1024)S(1)}, s32[65536]{0:T(1024)}, u32[]{:S(2)}) copy-start(s32[65536]{0:T(1024)} %param.6) | copy-start | bytes 786436
  2551.6 26.4 copy-start.5
  2578.0 33.7 %copy-start.6 = (f32[128]{0:T(128)}, f32[128]{0:T(128)S(1)}, u32[]{:S(2)}) copy-start(f32[128]{0:T(128)S(1)} %add_sqrt_fusion) | copy-start | bytes 1540
Sparse Core Ops, SparseCore 0:
  924.0 141.4 all-reduce.2
where the time goes:
time: 2650 us; the launch traced here: 2640 us
  waiting for transfers between devices  829 us (31%)
  blocking collectives  761 us (29%)
  local copies, waits for them, and re-layouts  424 us (16%)
  matrix products  317 us (12%)
  other arithmetic  282 us (11%)
    all_to_all x1, blocking collectives, local(): lax.all_to_all(coeffs, 'band', split_axis=1, concat_axis=0, tiled=True)  735 us
    all_to_all x1, waiting for transfers between devices, local(): lax.all_to_all(ortho_cols, 'band', split_axis=0, concat_axis=1, tiled=True)  687 us
    gather x1, local copies, waits for them, and re-layouts, local(): aligned = jnp.take(ortho, index_map, axis=1)  228 us
    another operation x15, matrix products, local(): lax.linalg.triangular_solve(factor, columns, left_side=True, lower=True)  177 us
    another operation x30, other arithmetic, local(): factor = jnp.linalg.cholesky(margin)  172 us
    psum x1, waiting for transfers between devices, local(): margin = lax.psum(partial_value, ('band', 'coef'))  142 us
    dot_general x1, matrix products, local(): jnp.dot(columns, columns.T, precision=lax.Precision.HIGHEST, preferred_el...  117 us
    unnamed x17, local copies, waits for them, and re-layouts  102 us
  transfers between devices with their start and end apart: 2, of which 2 were waited for; matrix products, arithmetic and copies ran while one was open for 1% of the time, Pallas kernels for 0%

commit v1 on v0

v1 whole, which is shorter than its diff:
```python
import functools
import jax
import jax.numpy as jnp
from jax import lax
from jax.experimental import pallas as pl
from jax.experimental.pallas import tpu as pltpu
from jax.sharding import PartitionSpec as P


NGROUPS = 16
UNITS = 16
PIECES = (2, 5, 5, 3, 1)
STAGES = (
    ("across", 1),
    ("within", 0),
    ("across", 2),
    ("added", 0),
    ("across", 3),
    ("within", 1),
    ("within", 2),
    ("across", 4),
    ("within", 3),
    ("within", 4),
)
TILE = 128
ROWS = 256
RANK = 4
STRETCH = 2048
UNROLL = 32
HIGHEST = lax.Precision.HIGHEST


def dot(a, b, dims):
    return lax.dot_general(a, b, (dims, ((), ())), precision=HIGHEST, preferred_element_type=jnp.float32)


def inverse_factor_kernel(packed_ref, out_ref, work, left, right):
    size = out_ref.shape[0]
    start = 0
    for index in range(size // ROWS):
        width = (index + 1) * ROWS
        work[index * ROWS:(index + 1) * ROWS, :width] = packed_ref[:, start:start + width]
        start += width
    rows = lax.broadcasted_iota(jnp.int32, (TILE, TILE), 0)
    lanes = lax.broadcasted_iota(jnp.int32, (TILE, TILE), 1)
    row_lanes = lax.broadcasted_iota(jnp.int32, (1, TILE), 1)
    tall_rows = lax.broadcasted_iota(jnp.int32, (size, TILE), 0)
    wide_lanes = lax.broadcasted_iota(jnp.int32, (TILE, size), 1)

    def block(index, carry):
        base = pl.multiple_of(index * TILE, TILE)
        left[...] = work[pl.ds(base, TILE), pl.ds(base, TILE)]
        right[...] = jnp.where(rows == lanes, 1.0, 0.0).astype(jnp.float32)

        def eliminate(step, inner):
            first = step * RANK
            current = left[...]
            strips = [left[pl.ds(first + t, 1), :] for t in range(RANK)]
            others = [right[pl.ds(first + t, 1), :] for t in range(RANK)]
            cols = [
                jnp.sum(jnp.where(lanes == first + t, current, 0.0), axis=1, keepdims=True)
                for t in range(RANK)
            ]
            core = [
                [
                    jnp.sum(jnp.where(row_lanes == first + u, strips[t], 0.0), axis=1, keepdims=True)
                    for u in range(RANK)
                ]
                for t in range(RANK)
            ]
            updated = right[...]
            for t in range(RANK):
                reciprocal = 1.0 / core[t][t]
                factor = jnp.where(rows > first + t, cols[t] * reciprocal, 0.0)
                for u in range(t + 1, RANK):
                    cols[u] = cols[u] - cols[t] * (reciprocal * core[t][u])
                    ratio = core[u][t] * reciprocal
                    strips[u] = strips[u] - ratio * strips[t]
                    others[u] = others[u] - ratio * others[t]
                    for v in range(t + 1, RANK):
                        core[u][v] = core[u][v] - ratio * core[t][v]
                current = current - factor * strips[t]
                updated = updated - factor * others[t]
            left[...] = current
            right[...] = updated
            return inner

        lax.fori_loop(0, TILE // RANK, eliminate, 0)
        pivots = jnp.sum(jnp.where(rows == lanes, left[...], 0.0), axis=1, keepdims=True)
        scale = lax.rsqrt(pivots)
        scale = scale * (1.5 - 0.5 * pivots * scale * scale)
        corner = right[...] * scale
        panel = dot(work[:, pl.ds(base, TILE)], corner, ((1,), (1,)))
        panel = jnp.where(tall_rows >= base + TILE, panel, 0.0)
        strip = jnp.where(wide_lanes < base, work[pl.ds(base, TILE), :], 0.0)
        strip = dot(corner, strip, ((1,), (0,)))
        work[:, pl.ds(base, TILE)] = jnp.zeros((size, TILE), jnp.float32)
        work[pl.ds(base, TILE), :] = strip
        work[pl.ds(base, TILE), pl.ds(base, TILE)] = corner
        strip = work[pl.ds(base, TILE), :] + panel.T
        work[...] = work[...] - dot(panel, strip, ((1,), (0,)))
        return carry

    lax.fori_loop(0, size // TILE, block, 0)
    shape = (size, size)
    below = lax.broadcasted_iota(jnp.int32, shape, 0) >= lax.broadcasted_iota(jnp.int32, shape, 1)
    out_ref[...] = jnp.where(below, work[...], 0.0)


def inverse_factor(packed, size):
    return pl.pallas_call(
        inverse_factor_kernel,
        out_shape=jax.ShapeDtypeStruct((size, size), jnp.float32),
        in_specs=[pl.BlockSpec(memory_space=pltpu.VMEM)],
        out_specs=pl.BlockSpec(memory_space=pltpu.VMEM),
        scratch_shapes=[
            pltpu.VMEM((size, size), jnp.float32),
            pltpu.VMEM((TILE, TILE), jnp.float32),
            pltpu.VMEM((TILE, TILE), jnp.float32),
        ],
        compiler_params=pltpu.CompilerParams(vmem_limit_bytes=48 * 1024 * 1024),
        name="inverse_factor",
    )(packed)


def rearrange_kernel(index_ref, block_ref, out_ref, table, turned):
    step = pl.program_id(0)
    count = pl.num_programs(0) // 2
    stretch = turned.shape[0]

    @pl.when(step < count)
    def scatter():
        turned[...] = block_ref[...].T

        def group(number, carry):
            base = pl.multiple_of(number * UNROLL, UNROLL)
            for t in range(UNROLL):
                table[pl.ds(index_ref[base + t], 1), :] = turned[pl.ds(base + t, 1), :]
            return carry

        lax.fori_loop(0, stretch // UNROLL, group, 0)

    @pl.when(step >= count)
    def write():
        base = pl.multiple_of((step - count) * stretch, stretch)
        out_ref[...] = table[pl.ds(base, stretch), :].T


def rearrange(index_map, values):
    bands, width = values.shape
    count = width // STRETCH
    return pl.pallas_call(
        rearrange_kernel,
        grid=(2 * count,),
        out_shape=jax.ShapeDtypeStruct(values.shape, values.dtype),
        in_specs=[
            pl.BlockSpec((STRETCH,), lambda i: (jnp.minimum(i, count - 1),), memory_space=pltpu.SMEM),
            pl.BlockSpec((bands, STRETCH), lambda i: (0, jnp.minimum(i, count - 1))),
        ],
        out_specs=pl.BlockSpec((bands, STRETCH), lambda i: (0, jnp.maximum(i - count, 0))),
        scratch_shapes=[
            pltpu.VMEM((width, bands), values.dtype),
            pltpu.VMEM((STRETCH, bands), values.dtype),
        ],
        compiler_params=pltpu.CompilerParams(vmem_limit_bytes=48 * 1024 * 1024),
        name="rearrange",
    )(index_map, values)


def sum_everywhere(value, axes):
    trail = []
    for axis, count in axes:
        place, step = lax.axis_index(axis), 1
        while step < count:
            pairs = [(i, i ^ step) for i in range(count)]
            rows = value.shape[0] // 2
            high = lax.rem(place // step, 2) == 1
            given = lax.dynamic_slice_in_dim(value, jnp.where(high, 0, rows), rows, 0)
            kept = lax.dynamic_slice_in_dim(value, jnp.where(high, rows, 0), rows, 0)
            value = kept + lax.ppermute(given, axis, pairs)
            trail.append((axis, pairs, high))
            step *= 2
    for axis, pairs, high in reversed(trail):
        got = lax.ppermute(value, axis, pairs)
        first, second = jnp.where(high, got, value), jnp.where(high, value, got)
        value = jnp.concatenate([first, second], axis=0)
    return value


def sum_small(value, axes):
    for axis, count in axes:
        step = 1
        while step < count:
            value = value + lax.ppermute(value, axis, [(i, i ^ step) for i in range(count)])
            step *= 2
    return value


def local(axes, coeffs, ref_block, index_map, band_group):
    bands, width = coeffs.shape
    parts = dict(axes)["band"]
    half = parts // 2
    size = bands * parts
    own = width // parts
    unit = own // UNITS
    offsets = [sum(PIECES[:k]) * unit for k in range(len(PIECES))]
    widths = [piece * unit for piece in PIECES]
    extra = widths[0]
    me = lax.axis_index("band")
    place = lax.rem(me, half)
    lower = me >= half

    def shift(value, step):
        return lax.ppermute(value, "band", [(i, i ^ step) for i in range(parts)])

    def take(row, column, rows, columns):
        return lax.dynamic_slice(coeffs, (row, column), (rows, columns))

    def put(buffer, value, row, column):
        return lax.dynamic_update_slice(buffer, value, (row, column))

    moved = rearrange(index_map, ref_block)

    columns, total = [], None
    for k in range(len(PIECES)):
        buffer = jnp.zeros((size, widths[k]), jnp.float32)
        buffer = put(buffer, take(0, me * own + offsets[k], bands, widths[k]), me * bands, 0)
        for step in reversed(range(1, parts)):
            peer = me ^ step
            got = shift(take(0, peer * own + offsets[k], bands, widths[k]), step)
            buffer = put(buffer, got, peer * bands, 0)
        columns.append(buffer)
        blocks = [
            dot(buffer[i:i + ROWS], buffer[:i + ROWS], ((1,), (1,))) for i in range(0, size, ROWS)
        ]
        packed = jnp.concatenate(blocks, axis=1)
        total = packed if total is None else total + packed

    margin = sum_everywhere(total, axes)
    margin, early = lax.optimization_barrier((margin, columns[0][:size // 2]))
    upper = lax.ppermute(early, "band", [(i, i + half) for i in range(half)])

    partner = me ^ half
    side = jnp.zeros((size // 2, extra), jnp.float32)
    side = put(side, take(0, partner * own, bands, extra), place * bands, 0)
    for step in range(1, half):
        peer = me ^ step
        got = shift(take(0, (peer ^ half) * own, bands, extra), step)
        side = put(side, got, lax.rem(peer, half) * bands, 0)
    upper = jnp.where(lower, upper, side)

    inverse_l = inverse_factor(margin, size)
    begin = jnp.where(lower, size // 2, 0)
    mine = lax.dynamic_slice(inverse_l, (begin, 0), (size // 2, size))
    theirs = lax.dynamic_slice(inverse_l, (size // 2 - begin, 0), (size // 2, size))

    ortho = jnp.zeros((bands, width), jnp.float32)
    squares = jnp.zeros((bands,), jnp.float32)
    pieces = []

    def rows_of(value, peer):
        return lax.dynamic_slice(value, (lax.rem(peer, half) * bands, 0), (bands, value.shape[1]))

    sliced = None
    for kind, k in STAGES:
        factor = theirs if kind == "across" else mine
        operand = jnp.concatenate([upper, side], axis=0) if kind == "added" else columns[k]
        if sliced is not None:
            factor, sliced = lax.optimization_barrier((factor, sliced))
            pieces[-1][0] = sliced
        value = dot(factor, operand, ((1,), (0,)))
        steps = range(half, parts) if kind == "across" else range(half)
        sliced = lax.optimization_barrier([rows_of(value, me ^ step) for step in steps])
        flip = half if kind == "added" else 0
        pieces.append([sliced, steps, [(me ^ step ^ flip) * own + offsets[k] for step in steps]])
    for sliced, steps, places in pieces:
        values = [shift(part, step) if step else part for part, step in zip(sliced, steps)]
        values, squares = lax.optimization_barrier((values, squares))
        for value, column in zip(values, places):
            ortho = put(ortho, value, 0, column)
            target = lax.dynamic_slice(moved, (0, column), value.shape)
            squares = squares + jnp.sum((value - target) ** 2, axis=1)

    band_residual = jnp.sqrt(sum_small(squares, axes[:1]) + 1e-06)
    hot = band_group[None, :] == jnp.arange(NGROUPS, dtype=jnp.int32)[:, None]
    terms = jnp.sum(jnp.where(hot, band_residual[None, :], 0.0), axis=1)
    group_residual = sum_small(terms, axes[1:]) * (NGROUPS / size)
    return (ortho, band_residual, group_residual)


def run(axes, *arrays):
    return local(axes, *arrays)


def solution(mesh):
    return jax.shard_map(
        functools.partial(run, tuple((name, mesh.shape[name]) for name in ("coef", "band"))),
        mesh=mesh,
        in_specs=(P("band", "coef"), P("band", "coef"), P("coef"), P("band")),
        out_specs=(P("band", "coef"), P("band"), P()),
        check_vma=False,
    )
```

time: 2650 us -> 2110 us (0.80)
  blocking collectives: 761 us -> 0 us
  starting transfers between devices: 7.1 us -> 586 us
  local copies, waits for them, and re-layouts: 424 us -> 137 us
  other arithmetic: 282 us -> 41.3 us
  Pallas kernels: 0 us -> 184 us
  waiting for transfers between devices: 829 us -> 911 us
  matrix products: 317 us -> 248 us
    ppermute x0 -> x88, waiting for transfers between devices: none -> 911 us  [the longest x72 837 us: shift(): return lax.ppermute(value, 'band', [(i, i ^ step) for i in range(parts)])]
    all_to_all x1 -> x0, blocking collectives: 735 us -> none  [local(): lax.all_to_all(coeffs, 'band', split_axis=1, concat_axis=0, tiled=True)]
    all_to_all x1 -> x0, waiting for transfers between devices: 687 us -> none  [local(): lax.all_to_all(ortho_cols, 'band', split_axis=0, concat_axis=1, tiled=True)]
    ppermute x0 -> x88, starting transfers between devices: none -> 586 us  [the longest x72 570 us: shift(): return lax.ppermute(value, 'band', [(i, i ^ step) for i in range(parts)])]
    another operation x33 -> x0, other arithmetic: 256 us -> none  [the longest x30 172 us: local(): factor = jnp.linalg.cholesky(margin)]
    gather x1 -> x0, local copies, waits for them, and re-layouts: 228 us -> none  [local(): aligned = jnp.take(ortho, index_map, axis=1)]
    another operation x29 -> x0, matrix products: 200 us -> none  [the longest x15 177 us: local(): lax.linalg.triangular_solve(factor, columns, left_side=True, lower=True)]
    pallas_call x0 -> x2, Pallas kernels: none -> 184 us  [the longest x1 94.9 us: rearrange(): pl.pallas_call(rearrange_kernel, grid=(2 * count,), out_shape=jax.ShapeDt...]
  transfers between devices with their start and end apart: 2 -> 88, of which waited for: 2 -> 43; matrix products, arithmetic and copies ran while one was open for 1% -> 17% of each run, Pallas kernels for 0% -> 4%
where the time goes in v1:
time: 2110 us
  waiting for transfers between devices  911 us (43%)
  starting transfers between devices  586 us (28%)
  matrix products  248 us (12%)
  Pallas kernels  184 us (9%)
  local copies, waits for them, and re-layouts  137 us (6%)
  other arithmetic  41.3 us (2%)
    ppermute x72, waiting for transfers between devices, shift(): return lax.ppermute(value, 'band', [(i, i ^ step) for i in range(parts)])  837 us
    ppermute x72, starting transfers between devices, shift(): return lax.ppermute(value, 'band', [(i, i ^ step) for i in range(parts)])  570 us
    dot_general x30, matrix products, dot(): lax.dot_general(a, b, (dims, ((), ())), precision=HIGHEST, preferred_elem...  248 us
    pallas_call x1, Pallas kernels, rearrange(): pl.pallas_call(rearrange_kernel, grid=(2 * count,), out_shape=jax.ShapeDt...  94.9 us
    pallas_call x1, Pallas kernels, inverse_factor(): pl.pallas_call(inverse_factor_kernel, out_shape=jax.ShapeDtypeStruct((siz...  89.6 us
    dynamic_update_slice x69, local copies, waits for them, and re-layouts, put(): return lax.dynamic_update_slice(buffer, value, (row, column))  70.9 us
  transfers between devices with their start and end apart: 88, of which 43 were waited for; matrix products, arithmetic and copies ran while one was open for 17% of the time, Pallas kernels for 4%

profile of v1, /device:TPU:0, one launch (start us, length us, event | category | flops | bytes accessed | tf_op | source)
XLA Modules:
  0.0 2109.6 jit_solution(4646792582257966099)
XLA Ops:
  26.7 5.5 constant_dynamic-slice_fusion.57
  37.4 13.9 constant_dynamic-slice_fusion.64
  67.0 5.6 collective-permute-done.31
  72.6 11.8 collective-permute-done.32
  96.4 32.3 %collective-permute-done = f32[128,1024]{1,0:T(8,128)S(1)} collective-permute-done((f32[128,1024]{1,0:T(8,128)S(1)}, f32[128,1024]{1,0:T(8,128)S(1)}, u32[]{:S(2)}, u32[]{:S(2)}) %collective-permute-start) | collective-permute-done | bytes 524320 | tf_op jit(solution)/shard_map/ppermute | solution.py:214
  128.7 37.9 %collective-permute-start.5 = (f32[128,1024]{1,0:T(8,128)S(1)}, f32[128,1024]{1,0:T(8,128)S(1)}, u32[]{:S(2)}, u32[]{:S(2)}) collective-permute-start(f32[128,1024]{1,0:T(8,128)S(1)} %copy-done.29), channel_id=1, source_target_pairs={{0,8},{4,12},{8,0},{12,4},{16,24},{20,28},{24,16},{28,20},{1,9},{5... | collective-permute-start | bytes 1572872 | tf_op jit(solution)/shard_map/ppermute | solution.py:214
  176.8 6.3 collective-permute-done.5
  189.3 6.1 fusion.43
  207.9 38.6 %collective-permute-done.21 = f32[128,1536]{1,0:T(8,128)S(1)} collective-permute-done((f32[128,1536]{1,0:T(8,128)S(1)}, f32[128,1536]{1,0:T(8,128)S(1)}, u32[]{:S(2)}, u32[]{:S(2)}) %collective-permute-start.21) | collective-permute-done | bytes 786464 | tf_op jit(solution)/shard_map/ppermute | solution.py:214
  246.5 62.9 %collective-permute-start.25 = (f32[128,1536]{1,0:T(8,128)S(1)}, f32[128,1536]{1,0:T(8,128)S(1)}, u32[]{:S(2)}, u32[]{:S(2)}) collective-permute-start(f32[128,1536]{1,0:T(8,128)S(1)} %copy-done.22), channel_id=1, source_target_pairs={{0,12},{4,8},{8,4},{12,0},{16,28},{20,24},{24,20},{28,16},{1,13},{... | collective-permute-start | bytes 2359304 | tf_op jit(solution)/shard_map/ppermute | solution.py:214
  315.9 39.2 %collective-permute-done.25 = f32[128,1536]{1,0:T(8,128)S(1)} collective-permute-done((f32[128,1536]{1,0:T(8,128)S(1)}, f32[128,1536]{1,0:T(8,128)S(1)}, u32[]{:S(2)}, u32[]{:S(2)}) %collective-permute-start.25) | collective-permute-done | bytes 786464 | tf_op jit(solution)/shard_map/ppermute | solution.py:214
  356.0 12.8 collective-permute-done.26
  374.6 8.4 fusion.35
  383.0 7.0 fusion.8
  399.4 54.8 %collective-permute-done.14 = f32[128,2560]{1,0:T(8,128)S(1)} collective-permute-done((f32[128,2560]{1,0:T(8,128)S(1)}, f32[128,2560]{1,0:T(8,128)S(1)}, u32[]{:S(2)}, u32[]{:S(2)}) %collective-permute-start.14) | collective-permute-done | bytes 1310752 | tf_op jit(solution)/shard_map/ppermute | solution.py:214
  454.2 86.4 %collective-permute-start.18 = (f32[128,2560]{1,0:T(8,128)S(1)}, f32[128,2560]{1,0:T(8,128)S(1)}, u32[]{:S(2)}, u32[]{:S(2)}) collective-permute-start(f32[128,2560]{1,0:T(8,128)S(1)} %copy-done.12), channel_id=1, source_target_pairs={{0,12},{4,8},{8,4},{12,0},{16,28},{20,24},{24,20},{28,16},{1,13},{... | collective-permute-start | bytes 3932168 | tf_op jit(solution)/shard_map/ppermute | solution.py:214
  549.5 39.0 %collective-permute-done.18 = f32[128,2560]{1,0:T(8,128)S(1)} collective-permute-done((f32[128,2560]{1,0:T(8,128)S(1)}, f32[128,2560]{1,0:T(8,128)S(1)}, u32[]{:S(2)}, u32[]{:S(2)}) %collective-permute-start.18) | collective-permute-done | bytes 1310752 | tf_op jit(solution)/shard_map/ppermute | solution.py:214
  593.5 23.1 %collective-permute-done.19 = f32[128,2560]{1,0:T(8,128)S(1)} collective-permute-done((f32[128,2560]{1,0:T(8,128)S(1)}, f32[128,2560]{1,0:T(8,128)S(1)}, u32[]{:S(2)}, u32[]{:S(2)}) %collective-permute-start.19) | collective-permute-done | bytes 1310752 | tf_op jit(solution)/shard_map/ppermute | solution.py:214
  616.7 5.6 collective-permute-start.9
  624.8 25.2 %collective-permute-done.7 = f32[128,2560]{1,0:T(8,128)S(1)} collective-permute-done((f32[128,2560]{1,0:T(8,128)S(1)}, f32[128,2560]{1,0:T(8,128)S(1)}, u32[]{:S(2)}, u32[]{:S(2)}) %collective-permute-start.7) | collective-permute-done | bytes 1310752 | tf_op jit(solution)/shard_map/ppermute | solution.py:214
  651.1 26.1 %collective-permute-done.8 = f32[128,2560]{1,0:T(8,128)S(1)} collective-permute-done((f32[128,2560]{1,0:T(8,128)S(1)}, f32[128,2560]{1,0:T(8,128)S(1)}, u32[]{:S(2)}, u32[]{:S(2)}) %collective-permute-start.8) | collective-permute-done | bytes 1310752 | tf_op jit(solution)/shard_map/ppermute | solution.py:214
  677.2 63.5 %collective-permute-start.12 = (f32[128,2560]{1,0:T(8,128)S(1)}, f32[128,2560]{1,0:T(8,128)S(1)}, u32[]{:S(2)}, u32[]{:S(2)}) collective-permute-start(f32[128,2560]{1,0:T(8,128)S(1)} %copy-done.4), channel_id=1, source_target_pairs={{0,8},{4,12},{8,0},{12,4},{16,24},{20,28},{24,16},{28,20},{1,9},{5... | collective-permute-start | bytes 3932168 | tf_op jit(solution)/shard_map/ppermute | solution.py:214
  741.8 26.6 %collective-permute-done.9 = f32[128,2560]{1,0:T(8,128)S(1)} collective-permute-done((f32[128,2560]{1,0:T(8,128)S(1)}, f32[128,2560]{1,0:T(8,128)S(1)}, u32[]{:S(2)}, u32[]{:S(2)}) %collective-permute-start.9) | collective-permute-done | bytes 1310752 | tf_op jit(solution)/shard_map/ppermute | solution.py:214
  769.6 25.4 %collective-permute-done.10 = f32[128,2560]{1,0:T(8,128)S(1)} collective-permute-done((f32[128,2560]{1,0:T(8,128)S(1)}, f32[128,2560]{1,0:T(8,128)S(1)}, u32[]{:S(2)}, u32[]{:S(2)}) %collective-permute-start.10) | collective-permute-done | bytes 1310752 | tf_op jit(solution)/shard_map/ppermute | solution.py:214
  797.3 7.8 fusion.4
  805.1 17.2 collective-permute-done.12
  828.2 9.5 fusion
  837.8 12.3 fusion.18
  856.0 7.4 fusion.6
  863.4 10.2 fusion.2
  873.7 12.2 fusion.24
  895.7 15.3 collective-permute-done.36
  913.1 7.9 collective-permute-done.37
  928.6 5.5 collective-permute-done.39
  934.2 5.8 collective-permute-done.40
  946.2 6.4 collective-permute-done.42
  954.3 9.1 collective-permute-done.43
  967.2 94.9 %rearrange.1 = f32[128,65536]{1,0:T(8,128)} custom-call(s32[65536]{0:T(1024)S(1)} %copy-done, f32[128,65536]{1,0:T(8,128)} %block_ref.1), custom_call_target="tpu_custom_call" | custom-call | tf_op jit(solution)/shard_map/rearrange/pallas_call | solution.py:152
  1071.3 89.6 %inverse_factor.1 = f32[1024,1024]{1,0:T(8,128)} custom-call(f32[256,2560]{1,0:T(8,128)S(1)} %pad_maximum_fusion.packed_ref), custom_call_target="tpu_custom_call" | custom-call | tf_op jit(solution)/shard_map/inverse_factor/pallas_call | solution.py:111
  1167.0 20.1 fusion.58
  1187.4 9.1 fusion.59
  1204.4 20.0 fusion.60
  1224.7 116.8 %collective-permute-done.45 = f32[128,2560]{1,0:T(8,128)S(1)} collective-permute-done((f32[128,2560]{1,0:T(8,128)S(1)}, f32[128,2560]{1,0:T(8,128)S(1)}, u32[]{:S(2)}, u32[]{:S(2)}) %collective-permute-start.45) | collective-permute-done | bytes 1310752 | tf_op jit(solution)/shard_map/ppermute | solution.py:214
  1342.8 27.5 %collective-permute-done.46 = f32[128,2560]{1,0:T(8,128)S(1)} collective-permute-done((f32[128,2560]{1,0:T(8,128)S(1)}, f32[128,2560]{1,0:T(8,128)S(1)}, u32[]{:S(2)}, u32[]{:S(2)}) %collective-permute-start.46) | collective-permute-done | bytes 1310752 | tf_op jit(solution)/shard_map/ppermute | solution.py:214
  1370.4 53.9 %collective-permute-start.50 = (f32[128,1024]{1,0:T(8,128)S(1)}, f32[128,1024]{1,0:T(8,128)S(1)}, u32[]{:S(2)}, u32[]{:S(2)}) collective-permute-start(f32[128,1024]{1,0:T(8,128)S(1)} %get-tuple-element.160), channel_id=1, source_target_pairs={{0,8},{4,12},{8,0},{12,4},{16,24},{20,28},{24,16},{28,20},{1,9},{5... | collective-permute-start | bytes 1572872 | tf_op jit(solution)/shard_map/ppermute | solution.py:214
  1424.2 28.8 %collective-permute-start.51 = (f32[128,1024]{1,0:T(8,128)S(1)}, f32[128,1024]{1,0:T(8,128)S(1)}, u32[]{:S(2)}, u32[]{:S(2)}) collective-permute-start(f32[128,1024]{1,0:T(8,128)S(1)} %get-tuple-element.161), channel_id=1, source_target_pairs={{0,12},{4,8},{8,4},{12,0},{16,28},{20,24},{24,20},{28,16},{1,13},{... | collective-permute-start | bytes 1572872 | tf_op jit(solution)/shard_map/ppermute | solution.py:214
  1453.0 41.1 %collective-permute-start.52 = (f32[128,2560]{1,0:T(8,128)S(1)}, f32[128,2560]{1,0:T(8,128)S(1)}, u32[]{:S(2)}, u32[]{:S(2)}) collective-permute-start(f32[128,2560]{1,0:T(8,128)S(1)} %get-tuple-element.172), channel_id=1, source_target_pairs={{0,16},{4,20},{8,24},{12,28},{16,0},{20,4},{24,8},{28,12},{1,17},{... | collective-permute-start | bytes 3932168 | tf_op jit(solution)/shard_map/ppermute | solution.py:214
  1494.2 11.6 broadcast_in_dim.33
  1521.8 113.1 %collective-permute-done.52 = f32[128,2560]{1,0:T(8,128)S(1)} collective-permute-done((f32[128,2560]{1,0:T(8,128)S(1)}, f32[128,2560]{1,0:T(8,128)S(1)}, u32[]{:S(2)}, u32[]{:S(2)}) %collective-permute-start.52) | collective-permute-done | bytes 1310752 | tf_op jit(solution)/shard_map/ppermute | solution.py:214
  1634.9 28.9 %collective-permute-done.53 = f32[128,2560]{1,0:T(8,128)S(1)} collective-permute-done((f32[128,2560]{1,0:T(8,128)S(1)}, f32[128,2560]{1,0:T(8,128)S(1)}, u32[]{:S(2)}, u32[]{:S(2)}) %collective-permute-start.53) | collective-permute-done | bytes 1310752 | tf_op jit(solution)/shard_map/ppermute | solution.py:214
  1675.2 8.5 fusion.10
  1684.6 56.7 %collective-permute-start.61 = (f32[128,1024]{1,0:T(8,128)S(1)}, f32[128,1024]{1,0:T(8,128)S(1)}, u32[]{:S(2)}, u32[]{:S(2)}) collective-permute-start(f32[128,1024]{1,0:T(8,128)S(1)} %get-tuple-element.189), channel_id=1, source_target_pairs={{0,8},{4,12},{8,0},{12,4},{16,24},{20,28},{24,16},{28,20},{1,9},{5... | collective-permute-start | bytes 1572872 | tf_op jit(solution)/shard_map/ppermute | solution.py:214
  1742.0 12.6 fusion.61
  1754.9 19.9 fusion.62
  1775.2 20.2 fusion.63
  1802.6 12.7 fusion.65
  1828.8 55.6 %collective-permute-done.63 = f32[128,1536]{1,0:T(8,128)S(1)} collective-permute-done((f32[128,1536]{1,0:T(8,128)S(1)}, f32[128,1536]{1,0:T(8,128)S(1)}, u32[]{:S(2)}, u32[]{:S(2)}) %collective-permute-start.63) | collective-permute-done | bytes 786464 | tf_op jit(solution)/shard_map/ppermute | solution.py:214
  1884.4 17.1 collective-permute-done.64
  1903.6 47.2 %collective-permute-start.71 = (f32[128,2560]{1,0:T(8,128)S(1)}, f32[128,2560]{1,0:T(8,128)S(1)}, u32[]{:S(2)}, u32[]{:S(2)}) collective-permute-start(f32[128,2560]{1,0:T(8,128)S(1)} %get-tuple-element.231), channel_id=1, source_target_pairs={{0,8},{4,12},{8,0},{12,4},{16,24},{20,28},{24,16},{28,20},{1,9},{5... | collective-permute-start | bytes 3932168 | tf_op jit(solution)/shard_map/ppermute | solution.py:214
  1969.8 25.8 %collective-permute-done.71 = f32[128,2560]{1,0:T(8,128)S(1)} collective-permute-done((f32[128,2560]{1,0:T(8,128)S(1)}, f32[128,2560]{1,0:T(8,128)S(1)}, u32[]{:S(2)}, u32[]{:S(2)}) %collective-permute-start.71) | collective-permute-done | bytes 1310752 | tf_op jit(solution)/shard_map/ppermute | solution.py:214
  1997.0 26.8 %collective-permute-done.72 = f32[128,2560]{1,0:T(8,128)S(1)} collective-permute-done((f32[128,2560]{1,0:T(8,128)S(1)}, f32[128,2560]{1,0:T(8,128)S(1)}, u32[]{:S(2)}, u32[]{:S(2)}) %collective-permute-start.72) | collective-permute-done | bytes 1310752 | tf_op jit(solution)/shard_map/ppermute | solution.py:214
  2050.0 9.6 collective-permute-done.78
  2059.6 16.9 collective-permute-done.79
  2082.1 5.5 collective-permute-done.82
  (353 shorter events, 326.8 us)
Async XLA Ops:
  3.8 83.3 %collective-permute-start.34 = (f32[128,512]{1,0:T(8,128)}, f32[128,512]{1,0:T(8,128)}, u32[]{:S(2)}, u32[]{:S(2)}) collective-permute-start(f32[128,512]{1,0:T(8,128)} %get-tuple-element.331), channel_id=1, source_target_pairs={{0,4},{4,0},{8,12},{12,8},{16,20},{20,16},{24,28},{28,24},{1,5},{5... | collective-permute-start | bytes 786440 | tf_op jit(solution)/shard_map/ppermute | solution.py:214
  6.7 77.7 %collective-permute-start.33 = (f32[128,512]{1,0:T(8,128)}, f32[128,512]{1,0:T(8,128)}, u32[]{:S(2)}, u32[]{:S(2)}) collective-permute-start(f32[128,512]{1,0:T(8,128)} %get-tuple-element.332), channel_id=1, source_target_pairs={{0,8},{4,12},{8,0},{12,4},{16,24},{20,28},{24,16},{28,20},{1,9},{5... | collective-permute-start | bytes 786440 | tf_op jit(solution)/shard_map/ppermute | solution.py:214
  8.3 55.3 %collective-permute-start.30 = (f32[128,512]{1,0:T(8,128)}, f32[128,512]{1,0:T(8,128)}, u32[]{:S(2)}, u32[]{:S(2)}) collective-permute-start(f32[128,512]{1,0:T(8,128)} %get-tuple-element.335), channel_id=1, source_target_pairs={{0,20},{4,16},{8,28},{12,24},{16,4},{20,0},{24,12},{28,8},{1,21},{... | collective-permute-start | bytes 786440 | tf_op jit(solution)/shard_map/ppermute | solution.py:214
  10.9 51.1 %collective-permute-start.29 = (f32[128,512]{1,0:T(8,128)}, f32[128,512]{1,0:T(8,128)}, u32[]{:S(2)}, u32[]{:S(2)}) collective-permute-start(f32[128,512]{1,0:T(8,128)} %get-tuple-element.336), channel_id=1, source_target_pairs={{0,24},{4,28},{8,16},{12,20},{16,8},{20,12},{24,0},{28,4},{1,25},{... | collective-permute-start | bytes 786440 | tf_op jit(solution)/shard_map/ppermute | solution.py:214
  10.9 50.0 %collective-permute-start.28 = (f32[128,512]{1,0:T(8,128)}, f32[128,512]{1,0:T(8,128)}, u32[]{:S(2)}, u32[]{:S(2)}) collective-permute-start(f32[128,512]{1,0:T(8,128)} %get-tuple-element.337), channel_id=1, source_target_pairs={{0,28},{4,24},{8,20},{12,16},{16,12},{20,8},{24,4},{28,0},{1,29},{... | collective-permute-start | bytes 786440 | tf_op jit(solution)/shard_map/ppermute | solution.py:214
  63.6 108.5 %collective-permute-start.4 = (f32[128,1024]{1,0:T(8,128)}, f32[128,1024]{1,0:T(8,128)S(1)}, u32[]{:S(2)}, u32[]{:S(2)}) collective-permute-start(f32[128,1024]{1,0:T(8,128)} %get-tuple-element.323), channel_id=1, source_target_pairs={{0,12},{4,8},{8,4},{12,0},{16,28},{20,24},{24,20},{28,16},{1,13},{... | collective-permute-start | bytes 1572872 | tf_op jit(solution)/shard_map/ppermute | solution.py:214
  72.6 98.7 %collective-permute-start.3 = (f32[128,1024]{1,0:T(8,128)}, f32[128,1024]{1,0:T(8,128)S(1)}, u32[]{:S(2)}, u32[]{:S(2)}) collective-permute-start(f32[128,1024]{1,0:T(8,128)} %get-tuple-element.325), channel_id=1, source_target_pairs={{0,16},{4,20},{8,24},{12,28},{16,0},{20,4},{24,8},{28,12},{1,17},{... | collective-permute-start | bytes 1572872 | tf_op jit(solution)/shard_map/ppermute | solution.py:214
  84.4 85.5 %collective-permute-start.2 = (f32[128,1024]{1,0:T(8,128)}, f32[128,1024]{1,0:T(8,128)S(1)}, u32[]{:S(2)}, u32[]{:S(2)}) collective-permute-start(f32[128,1024]{1,0:T(8,128)} %get-tuple-element.326), channel_id=1, source_target_pairs={{0,20},{4,16},{8,28},{12,24},{16,4},{20,0},{24,12},{28,8},{1,21},{... | collective-permute-start | bytes 1572872 | tf_op jit(solution)/shard_map/ppermute | solution.py:214
  84.5 83.0 %collective-permute-start.1 = (f32[128,1024]{1,0:T(8,128)S(1)}, f32[128,1024]{1,0:T(8,128)S(1)}, u32[]{:S(2)}, u32[]{:S(2)}) collective-permute-start(f32[128,1024]{1,0:T(8,128)S(1)} %copy-done.30), channel_id=1, source_target_pairs={{0,24},{4,28},{8,16},{12,20},{16,8},{20,12},{24,0},{28,4},{1,25},{... | collective-permute-start | bytes 1572872 | tf_op jit(solution)/shard_map/ppermute | solution.py:214
  128.7 54.4 %collective-permute-start.5 = (f32[128,1024]{1,0:T(8,128)S(1)}, f32[128,1024]{1,0:T(8,128)S(1)}, u32[]{:S(2)}, u32[]{:S(2)}) collective-permute-start(f32[128,1024]{1,0:T(8,128)S(1)} %copy-done.29), channel_id=1, source_target_pairs={{0,8},{4,12},{8,0},{12,4},{16,24},{20,28},{24,16},{28,20},{1,9},{5... | collective-permute-start | bytes 1572872 | tf_op jit(solution)/shard_map/ppermute | solution.py:214
  169.9 200.5 %collective-permute-start.27 = (f32[128,1536]{1,0:T(8,128)S(1)}, f32[128,1536]{1,0:T(8,128)S(1)}, u32[]{:S(2)}, u32[]{:S(2)}) collective-permute-start(f32[128,1536]{1,0:T(8,128)S(1)} %copy-done.20), channel_id=1, source_target_pairs={{0,4},{4,0},{8,12},{12,8},{16,20},{20,16},{24,28},{28,24},{1,5},{5... | collective-permute-start | bytes 2359304 | tf_op jit(solution)/shard_map/ppermute | solution.py:214
  171.3 142.5 %collective-permute-start.24 = (f32[128,1536]{1,0:T(8,128)S(1)}, f32[128,1536]{1,0:T(8,128)S(1)}, u32[]{:S(2)}, u32[]{:S(2)}) collective-permute-start(f32[128,1536]{1,0:T(8,128)S(1)} %copy-done.23), channel_id=1, source_target_pairs={{0,16},{4,20},{8,24},{12,28},{16,0},{20,4},{24,8},{28,12},{1,17},{... | collective-permute-start | bytes 2359304 | tf_op jit(solution)/shard_map/ppermute | solution.py:214
  172.1 139.3 %collective-permute-start.23 = (f32[128,1536]{1,0:T(8,128)S(1)}, f32[128,1536]{1,0:T(8,128)S(1)}, u32[]{:S(2)}, u32[]{:S(2)}) collective-permute-start(f32[128,1536]{1,0:T(8,128)S(1)} %copy-done.24), channel_id=1, source_target_pairs={{0,20},{4,16},{8,28},{12,24},{16,4},{20,0},{24,12},{28,8},{1,21},{... | collective-permute-start | bytes 2359304 | tf_op jit(solution)/shard_map/ppermute | solution.py:214
  183.0 127.3 %collective-permute-start.22 = (f32[128,1536]{1,0:T(8,128)S(1)}, f32[128,1536]{1,0:T(8,128)S(1)}, u32[]{:S(2)}, u32[]{:S(2)}) collective-permute-start(f32[128,1536]{1,0:T(8,128)S(1)} %copy-done.25), channel_id=1, source_target_pairs={{0,24},{4,28},{8,16},{12,20},{16,8},{20,12},{24,0},{28,4},{1,25},{... | collective-permute-start | bytes 2359304 | tf_op jit(solution)/shard_map/ppermute | solution.py:214
  187.1 59.4 %collective-permute-start.21 = (f32[128,1536]{1,0:T(8,128)S(1)}, f32[128,1536]{1,0:T(8,128)S(1)}, u32[]{:S(2)}, u32[]{:S(2)}) collective-permute-start(f32[128,1536]{1,0:T(8,128)S(1)} %copy-done.26), channel_id=1, source_target_pairs={{0,28},{4,24},{8,20},{12,16},{16,12},{20,8},{24,4},{28,0},{1,29},{... | collective-permute-start | bytes 2359304 | tf_op jit(solution)/shard_map/ppermute | solution.py:214
  246.5 108.6 %collective-permute-start.25 = (f32[128,1536]{1,0:T(8,128)S(1)}, f32[128,1536]{1,0:T(8,128)S(1)}, u32[]{:S(2)}, u32[]{:S(2)}) collective-permute-start(f32[128,1536]{1,0:T(8,128)S(1)} %copy-done.22), channel_id=1, source_target_pairs={{0,12},{4,8},{8,4},{12,0},{16,28},{20,24},{24,20},{28,16},{1,13},{... | collective-permute-start | bytes 2359304 | tf_op jit(solution)/shard_map/ppermute | solution.py:214
  310.4 58.5 %collective-permute-start.26 = (f32[128,1536]{1,0:T(8,128)S(1)}, f32[128,1536]{1,0:T(8,128)S(1)}, u32[]{:S(2)}, u32[]{:S(2)}) collective-permute-start(f32[128,1536]{1,0:T(8,128)S(1)} %copy-done.21), channel_id=1, source_target_pairs={{0,8},{4,12},{8,0},{12,4},{16,24},{20,28},{24,16},{28,20},{1,9},{5... | collective-permute-start | bytes 2359304 | tf_op jit(solution)/shard_map/ppermute | solution.py:214
  311.4 312.1 %collective-permute-start.20 = (f32[128,2560]{1,0:T(8,128)S(1)}, f32[128,2560]{1,0:T(8,128)S(1)}, u32[]{:S(2)}, u32[]{:S(2)}) collective-permute-start(f32[128,2560]{1,0:T(8,128)S(1)} %copy-done.10), channel_id=1, source_target_pairs={{0,4},{4,0},{8,12},{12,8},{16,20},{20,16},{24,28},{28,24},{1,5},{5... | collective-permute-start | bytes 3932168 | tf_op jit(solution)/shard_map/ppermute | solution.py:214
  313.8 231.1 %collective-permute-start.17 = (f32[128,2560]{1,0:T(8,128)S(1)}, f32[128,2560]{1,0:T(8,128)S(1)}, u32[]{:S(2)}, u32[]{:S(2)}) collective-permute-start(f32[128,2560]{1,0:T(8,128)S(1)} %copy-done.13), channel_id=1, source_target_pairs={{0,16},{4,20},{8,24},{12,28},{16,0},{20,4},{24,8},{28,12},{1,17},{... | collective-permute-start | bytes 3932168 | tf_op jit(solution)/shard_map/ppermute | solution.py:214
  355.1 188.0 %collective-permute-start.16 = (f32[128,2560]{1,0:T(8,128)S(1)}, f32[128,2560]{1,0:T(8,128)S(1)}, u32[]{:S(2)}, u32[]{:S(2)}) collective-permute-start(f32[128,2560]{1,0:T(8,128)S(1)} %copy-done.14), channel_id=1, source_target_pairs={{0,20},{4,16},{8,28},{12,24},{16,4},{20,0},{24,12},{28,8},{1,21},{... | collective-permute-start | bytes 3932168 | tf_op jit(solution)/shard_map/ppermute | solution.py:214
  368.8 173.0 %collective-permute-start.15 = (f32[128,2560]{1,0:T(8,128)S(1)}, f32[128,2560]{1,0:T(8,128)S(1)}, u32[]{:S(2)}, u32[]{:S(2)}) collective-permute-start(f32[128,2560]{1,0:T(8,128)S(1)} %copy-done.15), channel_id=1, source_target_pairs={{0,24},{4,28},{8,16},{12,20},{16,8},{20,12},{24,0},{28,4},{1,25},{... | collective-permute-start | bytes 3932168 | tf_op jit(solution)/shard_map/ppermute | solution.py:214
  370.3 83.9 %collective-permute-start.14 = (f32[128,2560]{1,0:T(8,128)S(1)}, f32[128,2560]{1,0:T(8,128)S(1)}, u32[]{:S(2)}, u32[]{:S(2)}) collective-permute-start(f32[128,2560]{1,0:T(8,128)S(1)} %copy-done.16), channel_id=1, source_target_pairs={{0,28},{4,24},{8,20},{12,16},{16,12},{20,8},{24,4},{28,0},{1,29},{... | collective-permute-start | bytes 3932168 | tf_op jit(solution)/shard_map/ppermute | solution.py:214
  454.2 134.4 %collective-permute-start.18 = (f32[128,2560]{1,0:T(8,128)S(1)}, f32[128,2560]{1,0:T(8,128)S(1)}, u32[]{:S(2)}, u32[]{:S(2)}) collective-permute-start(f32[128,2560]{1,0:T(8,128)S(1)} %copy-done.12), channel_id=1, source_target_pairs={{0,12},{4,8},{8,4},{12,0},{16,28},{20,24},{24,20},{28,16},{1,13},{... | collective-permute-start | bytes 3932168 | tf_op jit(solution)/shard_map/ppermute | solution.py:214
  541.8 74.9 %collective-permute-start.19 = (f32[128,2560]{1,0:T(8,128)S(1)}, f32[128,2560]{1,0:T(8,128)S(1)}, u32[]{:S(2)}, u32[]{:S(2)}) collective-permute-start(f32[128,2560]{1,0:T(8,128)S(1)} %copy-done.11), channel_id=1, source_target_pairs={{0,8},{4,12},{8,0},{12,4},{16,24},{20,28},{24,16},{28,20},{1,9},{5... | collective-permute-start | bytes 3932168 | tf_op jit(solution)/shard_map/ppermute | solution.py:214
  543.1 307.0 %collective-permute-start.13 = (f32[128,2560]{1,0:T(8,128)S(1)}, f32[128,2560]{1,0:T(8,128)S(1)}, u32[]{:S(2)}, u32[]{:S(2)}) collective-permute-start(f32[128,2560]{1,0:T(8,128)S(1)} %get-tuple-element.355), channel_id=1, source_target_pairs={{0,4},{4,0},{8,12},{12,8},{16,20},{20,16},{24,28},{28,24},{1,5},{5... | collective-permute-start | bytes 3932168 | tf_op jit(solution)/shard_map/ppermute | solution.py:214
  544.9 105.0 %collective-permute-start.7 = (f32[128,2560]{1,0:T(8,128)S(1)}, f32[128,2560]{1,0:T(8,128)S(1)}, u32[]{:S(2)}, u32[]{:S(2)}) collective-permute-start(f32[128,2560]{1,0:T(8,128)S(1)} %copy-done.9), channel_id=1, source_target_pairs={{0,28},{4,24},{8,20},{12,16},{16,12},{20,8},{24,4},{28,0},{1,29},{... | collective-permute-start | bytes 3932168 | tf_op jit(solution)/shard_map/ppermute | solution.py:214
  588.6 88.6 %collective-permute-start.8 = (f32[128,2560]{1,0:T(8,128)S(1)}, f32[128,2560]{1,0:T(8,128)S(1)}, u32[]{:S(2)}, u32[]{:S(2)}) collective-permute-start(f32[128,2560]{1,0:T(8,128)S(1)} %copy-done.8), channel_id=1, source_target_pairs={{0,24},{4,28},{8,16},{12,20},{16,8},{20,12},{24,0},{28,4},{1,25},{... | collective-permute-start | bytes 3932168 | tf_op jit(solution)/shard_map/ppermute | solution.py:214
  616.7 151.7 %collective-permute-start.9 = (f32[128,2560]{1,0:T(8,128)S(1)}, f32[128,2560]{1,0:T(8,128)S(1)}, u32[]{:S(2)}, u32[]{:S(2)}) collective-permute-start(f32[128,2560]{1,0:T(8,128)S(1)} %copy-done.7), channel_id=1, source_target_pairs={{0,20},{4,16},{8,28},{12,24},{16,4},{20,0},{24,12},{28,8},{1,21},{... | collective-permute-start | bytes 3932168 | tf_op jit(solution)/shard_map/ppermute | solution.py:214
  623.5 171.4 %collective-permute-start.10 = (f32[128,2560]{1,0:T(8,128)S(1)}, f32[128,2560]{1,0:T(8,128)S(1)}, u32[]{:S(2)}, u32[]{:S(2)}) collective-permute-start(f32[128,2560]{1,0:T(8,128)S(1)} %copy-done.6), channel_id=1, source_target_pairs={{0,16},{4,20},{8,24},{12,28},{16,0},{20,4},{24,8},{28,12},{1,17},{... | collective-permute-start | bytes 3932168 | tf_op jit(solution)/shard_map/ppermute | solution.py:214
  649.9 146.2 %collective-permute-start.11 = (f32[128,2560]{1,0:T(8,128)S(1)}, f32[128,2560]{1,0:T(8,128)S(1)}, u32[]{:S(2)}, u32[]{:S(2)}) collective-permute-start(f32[128,2560]{1,0:T(8,128)S(1)} %copy-done.5), channel_id=1, source_target_pairs={{0,12},{4,8},{8,4},{12,0},{16,28},{20,24},{24,20},{28,16},{1,13},{... | collective-permute-start | bytes 3932168 | tf_op jit(solution)/shard_map/ppermute | solution.py:214
  677.2 145.0 %collective-permute-start.12 = (f32[128,2560]{1,0:T(8,128)S(1)}, f32[128,2560]{1,0:T(8,128)S(1)}, u32[]{:S(2)}, u32[]{:S(2)}) collective-permute-start(f32[128,2560]{1,0:T(8,128)S(1)} %copy-done.4), channel_id=1, source_target_pairs={{0,8},{4,12},{8,0},{12,4},{16,24},{20,28},{24,16},{28,20},{1,9},{5... | collective-permute-start | bytes 3932168 | tf_op jit(solution)/shard_map/ppermute | solution.py:214
  963.6 106.1 %collective-permute-start.44 = (f32[128,2560]{1,0:T(8,128)S(1)}, f32[128,2560]{1,0:T(8,128)}, u32[]{:S(2)}, u32[]{:S(2)}) collective-permute-start(f32[128,2560]{1,0:T(8,128)S(1)} %pad_maximum_fusion.1), channel_id=1, source_target_pairs={{0,1},{1,0},{2,3},{3,2},{4,5},{5,4},{6,7},{7,6},{8,9},{9,8},{10,11... | collective-permute-start | bytes 3932168 | tf_op jit(solution)/shard_map/ppermute | solution.py:184
  963.6 100.3 %collective-permute-start.57 = (f32[128,1024]{1,0:T(8,128)}, f32[128,1024]{1,0:T(8,128)}, u32[]{:S(2)}, u32[]{:S(2)}) collective-permute-start(f32[128,1024]{1,0:T(8,128)} %get-tuple-element.320), channel_id=1, source_target_pairs={{0,4},{4,0},{8,12},{12,8},{16,20},{20,16},{24,28},{28,24},{1,5},{5... | collective-permute-start | bytes 1572872 | tf_op jit(solution)/shard_map/ppermute | solution.py:214
  964.4 101.5 %collective-permute-start.58 = (f32[128,1024]{1,0:T(8,128)}, f32[128,1024]{1,0:T(8,128)}, u32[]{:S(2)}, u32[]{:S(2)}) collective-permute-start(f32[128,1024]{1,0:T(8,128)} %get-tuple-element.330), channel_id=1, source_target_pairs={{0,8},{4,12},{8,0},{12,4},{16,24},{20,28},{24,16},{28,20},{1,9},{5... | collective-permute-start | bytes 1572872 | tf_op jit(solution)/shard_map/ppermute | solution.py:214
  966.4 101.3 %collective-permute-start.59 = (f32[128,1024]{1,0:T(8,128)S(1)}, f32[128,1024]{1,0:T(8,128)}, u32[]{:S(2)}, u32[]{:S(2)}) collective-permute-start(f32[128,1024]{1,0:T(8,128)S(1)} %copy-done.27), channel_id=1, source_target_pairs={{0,12},{4,8},{8,4},{12,0},{16,28},{20,24},{24,20},{28,16},{1,13},{... | collective-permute-start | bytes 1572872 | tf_op jit(solution)/shard_map/ppermute | solution.py:214
  1161.0 512.3 %collective-permute-start.56 = (f32[512,1024]{1,0:T(8,128)S(1)}, f32[512,1024]{1,0:T(8,128)S(1)}, u32[]{:S(2)}, u32[]{:S(2)}) collective-permute-start(f32[512,1024]{1,0:T(8,128)S(1)} %slice.128), channel_id=1, source_target_pairs={{0,16},{4,20},{8,24},{12,28},{1,17},{5,21},{9,25},{13,29},{2,18},{... | collective-permute-start | bytes 6291464 | tf_op jit(solution)/shard_map/ppermute | solution.py:241
  1196.7 144.9 %collective-permute-start.45 = (f32[128,2560]{1,0:T(8,128)S(1)}, f32[128,2560]{1,0:T(8,128)S(1)}, u32[]{:S(2)}, u32[]{:S(2)}) collective-permute-start(f32[128,2560]{1,0:T(8,128)S(1)} %get-tuple-element.145), channel_id=1, source_target_pairs={{0,16},{4,20},{8,24},{12,28},{16,0},{20,4},{24,8},{28,12},{1,17},{... | collective-permute-start | bytes 3932168 | tf_op jit(solution)/shard_map/ppermute | solution.py:214
  1196.7 173.6 %collective-permute-start.46 = (f32[128,2560]{1,0:T(8,128)S(1)}, f32[128,2560]{1,0:T(8,128)S(1)}, u32[]{:S(2)}, u32[]{:S(2)}) collective-permute-start(f32[128,2560]{1,0:T(8,128)S(1)} %get-tuple-element.146), channel_id=1, source_target_pairs={{0,20},{4,16},{8,28},{12,24},{16,4},{20,0},{24,12},{28,8},{1,21},{... | collective-permute-start | bytes 3932168 | tf_op jit(solution)/shard_map/ppermute | solution.py:214
  1200.4 223.8 %collective-permute-start.47 = (f32[128,2560]{1,0:T(8,128)S(1)}, f32[128,2560]{1,0:T(8,128)S(1)}, u32[]{:S(2)}, u32[]{:S(2)}) collective-permute-start(f32[128,2560]{1,0:T(8,128)S(1)} %get-tuple-element.147), channel_id=1, source_target_pairs={{0,24},{4,28},{8,16},{12,20},{16,8},{20,12},{24,0},{28,4},{1,25},{... | collective-permute-start | bytes 3932168 | tf_op jit(solution)/shard_map/ppermute | solution.py:214
  1201.9 251.1 %collective-permute-start.48 = (f32[128,2560]{1,0:T(8,128)S(1)}, f32[128,2560]{1,0:T(8,128)S(1)}, u32[]{:S(2)}, u32[]{:S(2)}) collective-permute-start(f32[128,2560]{1,0:T(8,128)S(1)} %get-tuple-element.148), channel_id=1, source_target_pairs={{0,28},{4,24},{8,20},{12,16},{16,12},{20,8},{24,4},{28,0},{1,29},{... | collective-permute-start | bytes 3932168 | tf_op jit(solution)/shard_map/ppermute | solution.py:214
  1341.5 169.7 %collective-permute-start.49 = (f32[128,1024]{1,0:T(8,128)S(1)}, f32[128,1024]{1,0:T(8,128)S(1)}, u32[]{:S(2)}, u32[]{:S(2)}) collective-permute-start(f32[128,1024]{1,0:T(8,128)S(1)} %get-tuple-element.159), channel_id=1, source_target_pairs={{0,4},{4,0},{8,12},{12,8},{16,20},{20,16},{24,28},{28,24},{1,5},{5... | collective-permute-start | bytes 1572872 | tf_op jit(solution)/shard_map/ppermute | solution.py:214
  1370.4 141.1 %collective-permute-start.50 = (f32[128,1024]{1,0:T(8,128)S(1)}, f32[128,1024]{1,0:T(8,128)S(1)}, u32[]{:S(2)}, u32[]{:S(2)}) collective-permute-start(f32[128,1024]{1,0:T(8,128)S(1)} %get-tuple-element.160), channel_id=1, source_target_pairs={{0,8},{4,12},{8,0},{12,4},{16,24},{20,28},{24,16},{28,20},{1,9},{5... | collective-permute-start | bytes 1572872 | tf_op jit(solution)/shard_map/ppermute | solution.py:214
  1424.2 87.5 %collective-permute-start.51 = (f32[128,1024]{1,0:T(8,128)S(1)}, f32[128,1024]{1,0:T(8,128)S(1)}, u32[]{:S(2)}, u32[]{:S(2)}) collective-permute-start(f32[128,1024]{1,0:T(8,128)S(1)} %get-tuple-element.161), channel_id=1, source_target_pairs={{0,12},{4,8},{8,4},{12,0},{16,28},{20,24},{24,20},{28,16},{1,13},{... | collective-permute-start | bytes 1572872 | tf_op jit(solution)/shard_map/ppermute | solution.py:214
  1453.0 181.9 %collective-permute-start.52 = (f32[128,2560]{1,0:T(8,128)S(1)}, f32[128,2560]{1,0:T(8,128)S(1)}, u32[]{:S(2)}, u32[]{:S(2)}) collective-permute-start(f32[128,2560]{1,0:T(8,128)S(1)} %get-tuple-element.172), channel_id=1, source_target_pairs={{0,16},{4,20},{8,24},{12,28},{16,0},{20,4},{24,8},{28,12},{1,17},{... | collective-permute-start | bytes 3932168 | tf_op jit(solution)/shard_map/ppermute | solution.py:214
  1511.3 152.5 %collective-permute-start.53 = (f32[128,2560]{1,0:T(8,128)S(1)}, f32[128,2560]{1,0:T(8,128)S(1)}, u32[]{:S(2)}, u32[]{:S(2)}) collective-permute-start(f32[128,2560]{1,0:T(8,128)S(1)} %get-tuple-element.173), channel_id=1, source_target_pairs={{0,20},{4,16},{8,28},{12,24},{16,4},{20,0},{24,12},{28,8},{1,21},{... | collective-permute-start | bytes 3932168 | tf_op jit(solution)/shard_map/ppermute | solution.py:214
  1511.5 152.3 %collective-permute-start.54 = (f32[128,2560]{1,0:T(8,128)S(1)}, f32[128,2560]{1,0:T(8,128)S(1)}, u32[]{:S(2)}, u32[]{:S(2)}) collective-permute-start(f32[128,2560]{1,0:T(8,128)S(1)} %get-tuple-element.174), channel_id=1, source_target_pairs={{0,24},{4,28},{8,16},{12,20},{16,8},{20,12},{24,0},{28,4},{1,25},{... | collective-permute-start | bytes 3932168 | tf_op jit(solution)/shard_map/ppermute | solution.py:214
  1511.7 152.1 %collective-permute-start.55 = (f32[128,2560]{1,0:T(8,128)S(1)}, f32[128,2560]{1,0:T(8,128)S(1)}, u32[]{:S(2)}, u32[]{:S(2)}) collective-permute-start(f32[128,2560]{1,0:T(8,128)S(1)} %get-tuple-element.175), channel_id=1, source_target_pairs={{0,28},{4,24},{8,20},{12,16},{16,12},{20,8},{24,4},{28,0},{1,29},{... | collective-permute-start | bytes 3932168 | tf_op jit(solution)/shard_map/ppermute | solution.py:214
  1683.9 135.3 %collective-permute-start.60 = (f32[128,1024]{1,0:T(8,128)S(1)}, f32[128,1024]{1,0:T(8,128)S(1)}, u32[]{:S(2)}, u32[]{:S(2)}) collective-permute-start(f32[128,1024]{1,0:T(8,128)S(1)} %get-tuple-element.188), channel_id=1, source_target_pairs={{0,4},{4,0},{8,12},{12,8},{16,20},{20,16},{24,28},{28,24},{1,5},{5... | collective-permute-start | bytes 1572872 | tf_op jit(solution)/shard_map/ppermute | solution.py:214
  1684.6 136.1 %collective-permute-start.61 = (f32[128,1024]{1,0:T(8,128)S(1)}, f32[128,1024]{1,0:T(8,128)S(1)}, u32[]{:S(2)}, u32[]{:S(2)}) collective-permute-start(f32[128,1024]{1,0:T(8,128)S(1)} %get-tuple-element.189), channel_id=1, source_target_pairs={{0,8},{4,12},{8,0},{12,4},{16,24},{20,28},{24,16},{28,20},{1,9},{5... | collective-permute-start | bytes 1572872 | tf_op jit(solution)/shard_map/ppermute | solution.py:214
  1741.3 82.5 %collective-permute-start.62 = (f32[128,1024]{1,0:T(8,128)S(1)}, f32[128,1024]{1,0:T(8,128)S(1)}, u32[]{:S(2)}, u32[]{:S(2)}) collective-permute-start(f32[128,1024]{1,0:T(8,128)S(1)} %get-tuple-element.190), channel_id=1, source_target_pairs={{0,12},{4,8},{8,4},{12,0},{16,28},{20,24},{24,20},{28,16},{1,13},{... | collective-permute-start | bytes 1572872 | tf_op jit(solution)/shard_map/ppermute | solution.py:214
  1795.8 88.6 %collective-permute-start.63 = (f32[128,1536]{1,0:T(8,128)S(1)}, f32[128,1536]{1,0:T(8,128)S(1)}, u32[]{:S(2)}, u32[]{:S(2)}) collective-permute-start(f32[128,1536]{1,0:T(8,128)S(1)} %get-tuple-element.201), channel_id=1, source_target_pairs={{0,16},{4,20},{8,24},{12,28},{16,0},{20,4},{24,8},{28,12},{1,17},{... | collective-permute-start | bytes 2359304 | tf_op jit(solution)/shard_map/ppermute | solution.py:214
  1795.9 105.6 %collective-permute-start.64 = (f32[128,1536]{1,0:T(8,128)S(1)}, f32[128,1536]{1,0:T(8,128)S(1)}, u32[]{:S(2)}, u32[]{:S(2)}) collective-permute-start(f32[128,1536]{1,0:T(8,128)S(1)} %get-tuple-element.202), channel_id=1, source_target_pairs={{0,20},{4,16},{8,28},{12,24},{16,4},{20,0},{24,12},{28,8},{1,21},{... | collective-permute-start | bytes 2359304 | tf_op jit(solution)/shard_map/ppermute | solution.py:214
  1819.2 83.2 %collective-permute-start.65 = (f32[128,1536]{1,0:T(8,128)S(1)}, f32[128,1536]{1,0:T(8,128)S(1)}, u32[]{:S(2)}, u32[]{:S(2)}) collective-permute-start(f32[128,1536]{1,0:T(8,128)S(1)} %get-tuple-element.203), channel_id=1, source_target_pairs={{0,24},{4,28},{8,16},{12,20},{16,8},{20,12},{24,0},{28,4},{1,25},{... | collective-permute-start | bytes 2359304 | tf_op jit(solution)/shard_map/ppermute | solution.py:214
  1820.8 82.8 %collective-permute-start.66 = (f32[128,1536]{1,0:T(8,128)S(1)}, f32[128,1536]{1,0:T(8,128)S(1)}, u32[]{:S(2)}, u32[]{:S(2)}) collective-permute-start(f32[128,1536]{1,0:T(8,128)S(1)} %get-tuple-element.204), channel_id=1, source_target_pairs={{0,28},{4,24},{8,20},{12,16},{16,12},{20,8},{24,4},{28,0},{1,29},{... | collective-permute-start | bytes 2359304 | tf_op jit(solution)/shard_map/ppermute | solution.py:214
  1823.8 132.0 %collective-permute-start.67 = (f32[128,2560]{1,0:T(8,128)S(1)}, f32[128,2560]{1,0:T(8,128)S(1)}, u32[]{:S(2)}, u32[]{:S(2)}) collective-permute-start(f32[128,2560]{1,0:T(8,128)S(1)} %get-tuple-element.216), channel_id=1, source_target_pairs={{0,4},{4,0},{8,12},{12,8},{16,20},{20,16},{24,28},{28,24},{1,5},{5... | collective-permute-start | bytes 3932168 | tf_op jit(solution)/shard_map/ppermute | solution.py:214
  1884.4 73.1 %collective-permute-start.68 = (f32[128,2560]{1,0:T(8,128)S(1)}, f32[128,2560]{1,0:T(8,128)S(1)}, u32[]{:S(2)}, u32[]{:S(2)}) collective-permute-start(f32[128,2560]{1,0:T(8,128)S(1)} %get-tuple-element.217), channel_id=1, source_target_pairs={{0,8},{4,12},{8,0},{12,4},{16,24},{20,28},{24,16},{28,20},{1,9},{5... | collective-permute-start | bytes 3932168 | tf_op jit(solution)/shard_map/ppermute | solution.py:214
  1901.5 58.3 %collective-permute-start.69 = (f32[128,2560]{1,0:T(8,128)S(1)}, f32[128,2560]{1,0:T(8,128)S(1)}, u32[]{:S(2)}, u32[]{:S(2)}) collective-permute-start(f32[128,2560]{1,0:T(8,128)S(1)} %get-tuple-element.218), channel_id=1, source_target_pairs={{0,12},{4,8},{8,4},{12,0},{16,28},{20,24},{24,20},{28,16},{1,13},{... | collective-permute-start | bytes 3932168 | tf_op jit(solution)/shard_map/ppermute | solution.py:214
  1902.4 64.6 %collective-permute-start.70 = (f32[128,2560]{1,0:T(8,128)S(1)}, f32[128,2560]{1,0:T(8,128)S(1)}, u32[]{:S(2)}, u32[]{:S(2)}) collective-permute-start(f32[128,2560]{1,0:T(8,128)S(1)} %get-tuple-element.230), channel_id=1, source_target_pairs={{0,4},{4,0},{8,12},{12,8},{16,20},{20,16},{24,28},{28,24},{1,5},{5... | collective-permute-start | bytes 3932168 | tf_op jit(solution)/shard_map/ppermute | solution.py:214
  1903.6 92.0 %collective-permute-start.71 = (f32[128,2560]{1,0:T(8,128)S(1)}, f32[128,2560]{1,0:T(8,128)S(1)}, u32[]{:S(2)}, u32[]{:S(2)}) collective-permute-start(f32[128,2560]{1,0:T(8,128)S(1)} %get-tuple-element.231), channel_id=1, source_target_pairs={{0,8},{4,12},{8,0},{12,4},{16,24},{20,28},{24,16},{28,20},{1,9},{5... | collective-permute-start | bytes 3932168 | tf_op jit(solution)/shard_map/ppermute | solution.py:214
  1955.8 68.0 %collective-permute-start.72 = (f32[128,2560]{1,0:T(8,128)S(1)}, f32[128,2560]{1,0:T(8,128)S(1)}, u32[]{:S(2)}, u32[]{:S(2)}) collective-permute-start(f32[128,2560]{1,0:T(8,128)S(1)} %get-tuple-element.232), channel_id=1, source_target_pairs={{0,12},{4,8},{8,4},{12,0},{16,28},{20,24},{24,20},{28,16},{1,13},{... | collective-permute-start | bytes 3932168 | tf_op jit(solution)/shard_map/ppermute | solution.py:214
  1957.5 77.7 %collective-permute-start.73 = (f32[128,512]{1,0:T(8,128)S(1)}, f32[128,512]{1,0:T(8,128)S(1)}, u32[]{:S(2)}, u32[]{:S(2)}) collective-permute-start(f32[128,512]{1,0:T(8,128)S(1)} %get-tuple-element.243), channel_id=1, source_target_pairs={{0,16},{4,20},{8,24},{12,28},{16,0},{20,4},{24,8},{28,12},{1,17},{... | collective-permute-start | bytes 786440 | tf_op jit(solution)/shard_map/ppermute | solution.py:214
  1959.9 75.3 %collective-permute-start.74 = (f32[128,512]{1,0:T(8,128)S(1)}, f32[128,512]{1,0:T(8,128)S(1)}, u32[]{:S(2)}, u32[]{:S(2)}) collective-permute-start(f32[128,512]{1,0:T(8,128)S(1)} %get-tuple-element.244), channel_id=1, source_target_pairs={{0,20},{4,16},{8,28},{12,24},{16,4},{20,0},{24,12},{28,8},{1,21},{... | collective-permute-start | bytes 786440 | tf_op jit(solution)/shard_map/ppermute | solution.py:214
  1966.9 71.8 %collective-permute-start.75 = (f32[128,512]{1,0:T(8,128)S(1)}, f32[128,512]{1,0:T(8,128)S(1)}, u32[]{:S(2)}, u32[]{:S(2)}) collective-permute-start(f32[128,512]{1,0:T(8,128)S(1)} %get-tuple-element.245), channel_id=1, source_target_pairs={{0,24},{4,28},{8,16},{12,20},{16,8},{20,12},{24,0},{28,4},{1,25},{... | collective-permute-start | bytes 786440 | tf_op jit(solution)/shard_map/ppermute | solution.py:214
  1995.6 48.8 %collective-permute-start.76 = (f32[128,512]{1,0:T(8,128)S(1)}, f32[128,512]{1,0:T(8,128)S(1)}, u32[]{:S(2)}, u32[]{:S(2)}) collective-permute-start(f32[128,512]{1,0:T(8,128)S(1)} %get-tuple-element.246), channel_id=1, source_target_pairs={{0,28},{4,24},{8,20},{12,16},{16,12},{20,8},{24,4},{28,0},{1,29},{... | collective-permute-start | bytes 786440 | tf_op jit(solution)/shard_map/ppermute | solution.py:214
  (58 other events, 1895.0 us)

commit v2 on v1

--- a/solution.py
+++ b/solution.py
@@ -9,17 +9,19 @@
 
 NGROUPS = 16
 UNITS = 16
-PIECES = (2, 5, 5, 3, 1)
+PIECES = (2, 5, 4, 3, 1, 1)
 STAGES = (
+    ("across", 5),
     ("across", 1),
     ("within", 0),
     ("across", 2),
     ("added", 0),
+    ("within", 1),
     ("across", 3),
-    ("within", 1),
     ("within", 2),
+    ("within", 3),
+    ("within", 5),
     ("across", 4),
-    ("within", 3),
     ("within", 4),
 )
 TILE = 128
@@ -167,24 +169,34 @@
     )(index_map, values)
 
 
-def sum_everywhere(value, axes):
+def sum_everywhere(value, hops):
     trail = []
-    for axis, count in axes:
-        place, step = lax.axis_index(axis), 1
-        while step < count:
-            pairs = [(i, i ^ step) for i in range(count)]
-            rows = value.shape[0] // 2
-            high = lax.rem(place // step, 2) == 1
-            given = lax.dynamic_slice_in_dim(value, jnp.where(high, 0, rows), rows, 0)
-            kept = lax.dynamic_slice_in_dim(value, jnp.where(high, rows, 0), rows, 0)
-            value = kept + lax.ppermute(given, axis, pairs)
-            trail.append((axis, pairs, high))
-            step *= 2
+    for axis, count, step in hops:
+        pairs = [(i, i ^ step) for i in range(count)]
+        rows = value.shape[0] // 2
+        high = lax.rem(lax.axis_index(axis) // step, 2) == 1
+        given = lax.dynamic_slice_in_dim(value, jnp.where(high, 0, rows), rows, 0)
+        kept = lax.dynamic_slice_in_dim(value, jnp.where(high, rows, 0), rows, 0)
+        value = kept + lax.ppermute(given, axis, pairs)
+        trail.append((axis, pairs, high))
     for axis, pairs, high in reversed(trail):
         got = lax.ppermute(value, axis, pairs)
         first, second = jnp.where(high, got, value), jnp.where(high, value, got)
         value = jnp.concatenate([first, second], axis=0)
     return value
+
+
+def sum_on_two_routes(value, axes):
+    hops = []
+    for axis, count in axes:
+        hops += [(axis, count, 1 << bit) for bit in range(count.bit_length() - 1)]
+    other = list(hops)
+    for k in range(1, len(hops) - 1, 2):
+        other[k], other[k + 1] = hops[k + 1], hops[k]
+    middle = value.shape[1] // 2
+    return jnp.concatenate(
+        [sum_everywhere(value[:, :middle], hops), sum_everywhere(value[:, middle:], other)], axis=1
+    )
 
 
 def sum_small(value, axes):
@@ -236,7 +248,7 @@
         packed = jnp.concatenate(blocks, axis=1)
         total = packed if total is None else total + packed
 
-    margin = sum_everywhere(total, axes)
+    margin = sum_on_two_routes(total, axes)
     margin, early = lax.optimization_barrier((margin, columns[0][:size // 2]))
     upper = lax.ppermute(early, "band", [(i, i + half) for i in range(half)])
 

time: 2110 us -> 2080 us (0.986)
  waiting for transfers between devices: 911 us -> 716 us
  starting transfers between devices: 586 us -> 720 us
    ppermute x72 -> x86, waiting for transfers between devices: 837 us -> 669 us  [shift(): return lax.ppermute(value, 'band', [(i, i ^ step) for i in range(parts)])]
    ppermute x72 -> x86, starting transfers between devices: 570 us -> 685 us  [shift(): return lax.ppermute(value, 'band', [(i, i ^ step) for i in range(parts)])]
    ppermute x5 -> x10, waiting for transfers between devices: 37.3 us -> 15.5 us  [sum_everywhere(): value = kept + lax.ppermute(given, axis, pairs)]
    dot_general x30 -> x36, matrix products: 248 us -> 256 us  [dot(): lax.dot_general(a, b, (dims, ((), ())), precision=HIGHEST, preferred_elem...]
    dynamic_update_slice x69 -> x82, local copies, waits for them, and re-layouts: 70.9 us -> 78.3 us  [put(): return lax.dynamic_update_slice(buffer, value, (row, column))]
  transfers between devices with their start and end apart: 88 -> 112, of which waited for: 43 -> 51; matrix products, arithmetic and copies ran while one was open for 17% -> 19% of each run, Pallas kernels for 4% -> 5%
where the time goes in v2:
time: 2080 us; the launch traced here: 2070 us
  starting transfers between devices  720 us (35%)
  waiting for transfers between devices  716 us (34%)
  matrix products  256 us (12%)
  Pallas kernels  185 us (9%)
  local copies, waits for them, and re-layouts  149 us (7%)
  other arithmetic  40.4 us (2%)
    ppermute x86, starting transfers between devices, shift(): return lax.ppermute(value, 'band', [(i, i ^ step) for i in range(parts)])  685 us
    ppermute x86, waiting for transfers between devices, shift(): return lax.ppermute(value, 'band', [(i, i ^ step) for i in range(parts)])  669 us
    dot_general x36, matrix products, dot(): lax.dot_general(a, b, (dims, ((), ())), precision=HIGHEST, preferred_elem...  256 us
    pallas_call x1, Pallas kernels, rearrange(): pl.pallas_call(rearrange_kernel, grid=(2 * count,), out_shape=jax.ShapeDt...  95.1 us
    pallas_call x1, Pallas kernels, inverse_factor(): pl.pallas_call(inverse_factor_kernel, out_shape=jax.ShapeDtypeStruct((siz...  89.7 us
    dynamic_update_slice x82, local copies, waits for them, and re-layouts, put(): return lax.dynamic_update_slice(buffer, value, (row, column))  78.3 us
  transfers between devices with their start and end apart: 112, of which 51 were waited for; matrix products, arithmetic and copies ran while one was open for 19% of the time, Pallas kernels for 5%

profile of v2, /device:TPU:0, one launch (start us, length us, event | category | flops | bytes accessed | tf_op | source)
XLA Modules:
  0.0 2068.9 jit_solution(13590607705917646934)
XLA Ops:
  20.2 5.4 constant_dynamic-slice_fusion.79
  30.1 6.9 constant_dynamic-slice_fusion.86
  42.2 7.7 constant_dynamic-slice_fusion.93
  74.0 15.5 collective-permute-start.38
  90.2 10.8 collective-permute-done.37
  101.1 8.5 collective-permute-done.30
  136.8 6.1 collective-permute-done.39
  164.4 22.4 %collective-permute-done = f32[128,1024]{1,0:T(8,128)S(1)} collective-permute-done((f32[128,1024]{1,0:T(8,128)S(1)}, f32[128,1024]{1,0:T(8,128)S(1)}, u32[]{:S(2)}, u32[]{:S(2)}) %collective-permute-start) | collective-permute-done | bytes 524320 | tf_op jit(solution)/shard_map/ppermute | solution.py:226
  186.9 37.4 %collective-permute-start.5 = (f32[128,1024]{1,0:T(8,128)S(1)}, f32[128,1024]{1,0:T(8,128)S(1)}, u32[]{:S(2)}, u32[]{:S(2)}) collective-permute-start(f32[128,1024]{1,0:T(8,128)S(1)} %copy-done.28), channel_id=1, source_target_pairs={{0,8},{4,12},{8,0},{12,4},{16,24},{20,28},{24,16},{28,20},{1,9},{5... | collective-permute-start | bytes 1572872 | tf_op jit(solution)/shard_map/ppermute | solution.py:226
  233.5 5.5 collective-permute-done.5
  245.2 5.9 fusion.48
  263.1 39.2 %collective-permute-done.21 = f32[128,1536]{1,0:T(8,128)S(1)} collective-permute-done((f32[128,1536]{1,0:T(8,128)S(1)}, f32[128,1536]{1,0:T(8,128)S(1)}, u32[]{:S(2)}, u32[]{:S(2)}) %collective-permute-start.21) | collective-permute-done | bytes 786464 | tf_op jit(solution)/shard_map/ppermute | solution.py:226
  302.3 63.7 %collective-permute-start.25 = (f32[128,1536]{1,0:T(8,128)S(1)}, f32[128,1536]{1,0:T(8,128)S(1)}, u32[]{:S(2)}, u32[]{:S(2)}) collective-permute-start(f32[128,1536]{1,0:T(8,128)S(1)} %copy-done.21), channel_id=1, source_target_pairs={{0,12},{4,8},{8,4},{12,0},{16,28},{20,24},{24,20},{28,16},{1,13},{... | collective-permute-start | bytes 2359304 | tf_op jit(solution)/shard_map/ppermute | solution.py:226
  371.9 46.2 %collective-permute-done.25 = f32[128,1536]{1,0:T(8,128)S(1)} collective-permute-done((f32[128,1536]{1,0:T(8,128)S(1)}, f32[128,1536]{1,0:T(8,128)S(1)}, u32[]{:S(2)}, u32[]{:S(2)}) %collective-permute-start.25) | collective-permute-done | bytes 786464 | tf_op jit(solution)/shard_map/ppermute | solution.py:226
  419.0 15.7 collective-permute-done.26
  441.2 8.4 fusion.38
  449.5 7.0 fusion.6
  466.0 45.2 %collective-permute-done.14 = f32[128,2048]{1,0:T(8,128)S(1)} collective-permute-done((f32[128,2048]{1,0:T(8,128)S(1)}, f32[128,2048]{1,0:T(8,128)S(1)}, u32[]{:S(2)}, u32[]{:S(2)}) %collective-permute-start.14) | collective-permute-done | bytes 1048608 | tf_op jit(solution)/shard_map/ppermute | solution.py:226
  511.3 57.9 %collective-permute-start.19 = (f32[128,2048]{1,0:T(8,128)S(1)}, f32[128,2048]{1,0:T(8,128)S(1)}, u32[]{:S(2)}, u32[]{:S(2)}) collective-permute-start(f32[128,2048]{1,0:T(8,128)S(1)} %copy-done.13), channel_id=1, source_target_pairs={{0,8},{4,12},{8,0},{12,4},{16,24},{20,28},{24,16},{28,20},{1,9},{5... | collective-permute-start | bytes 3145736 | tf_op jit(solution)/shard_map/ppermute | solution.py:226
  579.1 18.6 collective-permute-done.19
  602.6 10.2 fusion.28
  612.8 8.2 fusion.2
  621.1 6.8 fusion.8
  632.8 63.9 %collective-permute-done.7 = f32[128,2560]{1,0:T(8,128)S(1)} collective-permute-done((f32[128,2560]{1,0:T(8,128)S(1)}, f32[128,2560]{1,0:T(8,128)S(1)}, u32[]{:S(2)}, u32[]{:S(2)}) %collective-permute-start.7) | collective-permute-done | bytes 1310752 | tf_op jit(solution)/shard_map/ppermute | solution.py:226
  696.6 97.9 %collective-permute-start.11 = (f32[128,2560]{1,0:T(8,128)S(1)}, f32[128,2560]{1,0:T(8,128)S(1)}, u32[]{:S(2)}, u32[]{:S(2)}) collective-permute-start(f32[128,2560]{1,0:T(8,128)S(1)} %copy-done.5), channel_id=1, source_target_pairs={{0,12},{4,8},{8,4},{12,0},{16,28},{20,24},{24,20},{28,16},{1,13},{... | collective-permute-start | bytes 3932168 | tf_op jit(solution)/shard_map/ppermute | solution.py:226
  803.0 21.2 %collective-permute-done.11 = f32[128,2560]{1,0:T(8,128)S(1)} collective-permute-done((f32[128,2560]{1,0:T(8,128)S(1)}, f32[128,2560]{1,0:T(8,128)S(1)}, u32[]{:S(2)}, u32[]{:S(2)}) %collective-permute-start.11) | collective-permute-done | bytes 1310752 | tf_op jit(solution)/shard_map/ppermute | solution.py:226
  825.4 18.8 collective-permute-done.12
  851.3 7.4 fusion.4
  858.7 9.6 fusion
  868.3 12.3 fusion.18
  889.2 95.1 %rearrange.1 = f32[128,65536]{1,0:T(8,128)} custom-call(s32[65536]{0:T(1024)S(1)} %copy-done, f32[128,65536]{1,0:T(8,128)} %block_ref.1), custom_call_target="tpu_custom_call" | custom-call | tf_op jit(solution)/shard_map/rearrange/pallas_call | solution.py:154
  990.1 6.5 collective-permute-done.53
  1026.1 5.4 collective-permute-done.59
  1045.8 89.7 %inverse_factor.1 = f32[1024,1024]{1,0:T(8,128)} custom-call(f32[256,2560]{1,0:T(8,128)S(1)} %maximum_maximum_fusion.packed_ref), custom_call_target="tpu_custom_call" | custom-call | tf_op jit(solution)/shard_map/inverse_factor/pallas_call | solution.py:113
  1147.4 20.2 fusion.73
  1168.0 9.1 fusion.74
  1185.0 16.2 fusion.75
  1203.5 93.9 %collective-permute-done.65 = f32[128,512]{1,0:T(8,128)S(1)} collective-permute-done((f32[128,512]{1,0:T(8,128)S(1)}, f32[128,512]{1,0:T(8,128)S(1)}, u32[]{:S(2)}, u32[]{:S(2)}) %collective-permute-start.65) | collective-permute-done | bytes 262176 | tf_op jit(solution)/shard_map/ppermute | solution.py:226
  1299.4 11.2 broadcast_in_dim.36
  1314.7 11.2 collective-permute-done.66
  1326.0 107.3 %collective-permute-start.71 = (f32[128,1024]{1,0:T(8,128)S(1)}, f32[128,1024]{1,0:T(8,128)S(1)}, u32[]{:S(2)}, u32[]{:S(2)}) collective-permute-start(f32[128,1024]{1,0:T(8,128)S(1)} %get-tuple-element.202), channel_id=1, source_target_pairs={{0,8},{4,12},{8,0},{12,4},{16,24},{20,28},{24,16},{28,20},{1,9},{5... | collective-permute-start | bytes 1572872 | tf_op jit(solution)/shard_map/ppermute | solution.py:226
  1445.6 21.7 %collective-permute-done.71 = f32[128,1024]{1,0:T(8,128)S(1)} collective-permute-done((f32[128,1024]{1,0:T(8,128)S(1)}, f32[128,1024]{1,0:T(8,128)S(1)}, u32[]{:S(2)}, u32[]{:S(2)}) %collective-permute-start.71) | collective-permute-done | bytes 524320 | tf_op jit(solution)/shard_map/ppermute | solution.py:226
  1469.3 8.2 collective-permute-done.72
  1484.6 65.9 %collective-permute-done.73 = f32[128,2048]{1,0:T(8,128)S(1)} collective-permute-done((f32[128,2048]{1,0:T(8,128)S(1)}, f32[128,2048]{1,0:T(8,128)S(1)}, u32[]{:S(2)}, u32[]{:S(2)}) %collective-permute-start.73) | collective-permute-done | bytes 1048608 | tf_op jit(solution)/shard_map/ppermute | solution.py:226
  1550.5 23.1 %collective-permute-done.74 = f32[128,2048]{1,0:T(8,128)S(1)} collective-permute-done((f32[128,2048]{1,0:T(8,128)S(1)}, f32[128,2048]{1,0:T(8,128)S(1)}, u32[]{:S(2)}, u32[]{:S(2)}) %collective-permute-start.74) | collective-permute-done | bytes 1048608 | tf_op jit(solution)/shard_map/ppermute | solution.py:226
  1582.1 8.4 collective-permute-done.77
  1592.4 8.5 fusion.10
  1601.1 20.2 fusion.76
  1622.8 115.1 %collective-permute-start.82 = (f32[128,1024]{1,0:T(8,128)S(1)}, f32[128,1024]{1,0:T(8,128)S(1)}, u32[]{:S(2)}, u32[]{:S(2)}) collective-permute-start(f32[128,1024]{1,0:T(8,128)S(1)} %get-tuple-element.231), channel_id=1, source_target_pairs={{0,8},{4,12},{8,0},{12,4},{16,24},{20,28},{24,16},{28,20},{1,9},{5... | collective-permute-start | bytes 1572872 | tf_op jit(solution)/shard_map/ppermute | solution.py:226
  1741.4 12.6 fusion.77
  1754.2 16.0 fusion.78
  1770.8 12.7 fusion.79
  1811.0 33.2 %collective-permute-done.86 = f32[128,2560]{1,0:T(8,128)S(1)} collective-permute-done((f32[128,2560]{1,0:T(8,128)S(1)}, f32[128,2560]{1,0:T(8,128)S(1)}, u32[]{:S(2)}, u32[]{:S(2)}) %collective-permute-start.86) | collective-permute-done | bytes 1310752 | tf_op jit(solution)/shard_map/ppermute | solution.py:226
  1849.7 35.9 %collective-permute-start.98 = (f32[128,512]{1,0:T(8,128)S(1)}, f32[128,512]{1,0:T(8,128)S(1)}, u32[]{:S(2)}, u32[]{:S(2)}) collective-permute-start(f32[128,512]{1,0:T(8,128)S(1)} %get-tuple-element.301), channel_id=1, source_target_pairs={{0,8},{4,12},{8,0},{12,4},{16,24},{20,28},{24,16},{28,20},{1,9},{5... | collective-permute-start | bytes 786440 | tf_op jit(solution)/shard_map/ppermute | solution.py:226
  1885.6 19.6 collective-permute-done.88
  1906.5 15.9 collective-permute-start.92
  1922.5 14.1 collective-permute-start.93
  1943.8 14.1 collective-permute-start.95
  1957.9 7.8 collective-permute-done.93
  1974.7 5.8 collective-permute-done.94
  1983.6 16.6 collective-permute-done.96
  2018.7 9.5 collective-permute-done.100
  2028.3 7.0 collective-permute-done.101
  2055.3 6.6 collective-permute-start.110
  (454 shorter events, 411.9 us)
Async XLA Ops:
  5.0 148.5 %collective-permute-start.41 = (f32[128,512]{1,0:T(8,128)}, f32[128,512]{1,0:T(8,128)}, u32[]{:S(2)}, u32[]{:S(2)}) collective-permute-start(f32[128,512]{1,0:T(8,128)} %get-tuple-element.395), channel_id=1, source_target_pairs={{0,4},{4,0},{8,12},{12,8},{16,20},{20,16},{24,28},{28,24},{1,5},{5... | collective-permute-start | bytes 786440 | tf_op jit(solution)/shard_map/ppermute | solution.py:226
  8.0 139.6 %collective-permute-start.40 = (f32[128,512]{1,0:T(8,128)}, f32[128,512]{1,0:T(8,128)}, u32[]{:S(2)}, u32[]{:S(2)}) collective-permute-start(f32[128,512]{1,0:T(8,128)} %get-tuple-element.396), channel_id=1, source_target_pairs={{0,8},{4,12},{8,0},{12,4},{16,24},{20,28},{24,16},{28,20},{1,9},{5... | collective-permute-start | bytes 786440 | tf_op jit(solution)/shard_map/ppermute | solution.py:226
  9.6 57.4 %collective-permute-start.36 = (f32[128,512]{1,0:T(8,128)}, f32[128,512]{1,0:T(8,128)}, u32[]{:S(2)}, u32[]{:S(2)}) collective-permute-start(f32[128,512]{1,0:T(8,128)} %get-tuple-element.400), channel_id=1, source_target_pairs={{0,24},{4,28},{8,16},{12,20},{16,8},{20,12},{24,0},{28,4},{1,25},{... | collective-permute-start | bytes 786440 | tf_op jit(solution)/shard_map/ppermute | solution.py:226
  12.1 50.6 %collective-permute-start.35 = (f32[128,512]{1,0:T(8,128)}, f32[128,512]{1,0:T(8,128)}, u32[]{:S(2)}, u32[]{:S(2)}) collective-permute-start(f32[128,512]{1,0:T(8,128)} %get-tuple-element.401), channel_id=1, source_target_pairs={{0,28},{4,24},{8,20},{12,16},{16,12},{20,8},{24,4},{28,0},{1,29},{... | collective-permute-start | bytes 786440 | tf_op jit(solution)/shard_map/ppermute | solution.py:226
  13.4 51.8 %collective-permute-start.28 = (f32[128,512]{1,0:T(8,128)}, f32[128,512]{1,0:T(8,128)}, u32[]{:S(2)}, u32[]{:S(2)}) collective-permute-start(f32[128,512]{1,0:T(8,128)} %get-tuple-element.409), channel_id=1, source_target_pairs={{0,28},{4,24},{8,20},{12,16},{16,12},{20,8},{24,4},{28,0},{1,29},{... | collective-permute-start | bytes 786440 | tf_op jit(solution)/shard_map/ppermute | solution.py:226
  67.0 42.6 %collective-permute-start.30 = (f32[128,512]{1,0:T(8,128)}, f32[128,512]{1,0:T(8,128)S(1)}, u32[]{:S(2)}, u32[]{:S(2)}) collective-permute-start(f32[128,512]{1,0:T(8,128)} %get-tuple-element.407), channel_id=1, source_target_pairs={{0,20},{4,16},{8,28},{12,24},{16,4},{20,0},{24,12},{28,8},{1,21},{... | collective-permute-start | bytes 786440 | tf_op jit(solution)/shard_map/ppermute | solution.py:226
  74.0 40.9 %collective-permute-start.38 = (f32[128,512]{1,0:T(8,128)}, f32[128,512]{1,0:T(8,128)S(1)}, u32[]{:S(2)}, u32[]{:S(2)}) collective-permute-start(f32[128,512]{1,0:T(8,128)} %get-tuple-element.398), channel_id=1, source_target_pairs={{0,16},{4,20},{8,24},{12,28},{16,0},{20,4},{24,8},{28,12},{1,17},{... | collective-permute-start | bytes 786440 | tf_op jit(solution)/shard_map/ppermute | solution.py:226
  129.8 99.8 %collective-permute-start.4 = (f32[128,1024]{1,0:T(8,128)S(1)}, f32[128,1024]{1,0:T(8,128)S(1)}, u32[]{:S(2)}, u32[]{:S(2)}) collective-permute-start(f32[128,1024]{1,0:T(8,128)S(1)} %copy-done.29), channel_id=1, source_target_pairs={{0,12},{4,8},{8,4},{12,0},{16,28},{20,24},{24,20},{28,16},{1,13},{... | collective-permute-start | bytes 1572872 | tf_op jit(solution)/shard_map/ppermute | solution.py:226
  130.5 98.2 %collective-permute-start.3 = (f32[128,1024]{1,0:T(8,128)S(1)}, f32[128,1024]{1,0:T(8,128)S(1)}, u32[]{:S(2)}, u32[]{:S(2)}) collective-permute-start(f32[128,1024]{1,0:T(8,128)S(1)} %copy-done.30), channel_id=1, source_target_pairs={{0,16},{4,20},{8,24},{12,28},{16,0},{20,4},{24,8},{28,12},{1,17},{... | collective-permute-start | bytes 1572872 | tf_op jit(solution)/shard_map/ppermute | solution.py:226
  142.9 83.7 %collective-permute-start.2 = (f32[128,1024]{1,0:T(8,128)S(1)}, f32[128,1024]{1,0:T(8,128)S(1)}, u32[]{:S(2)}, u32[]{:S(2)}) collective-permute-start(f32[128,1024]{1,0:T(8,128)S(1)} %copy-done.31), channel_id=1, source_target_pairs={{0,20},{4,16},{8,28},{12,24},{16,4},{20,0},{24,12},{28,8},{1,21},{... | collective-permute-start | bytes 1572872 | tf_op jit(solution)/shard_map/ppermute | solution.py:226
  147.6 77.4 %collective-permute-start.1 = (f32[128,1024]{1,0:T(8,128)S(1)}, f32[128,1024]{1,0:T(8,128)S(1)}, u32[]{:S(2)}, u32[]{:S(2)}) collective-permute-start(f32[128,1024]{1,0:T(8,128)S(1)} %copy-done.32), channel_id=1, source_target_pairs={{0,24},{4,28},{8,16},{12,20},{16,8},{20,12},{24,0},{28,4},{1,25},{... | collective-permute-start | bytes 1572872 | tf_op jit(solution)/shard_map/ppermute | solution.py:226
  186.9 52.1 %collective-permute-start.5 = (f32[128,1024]{1,0:T(8,128)S(1)}, f32[128,1024]{1,0:T(8,128)S(1)}, u32[]{:S(2)}, u32[]{:S(2)}) collective-permute-start(f32[128,1024]{1,0:T(8,128)S(1)} %copy-done.28), channel_id=1, source_target_pairs={{0,8},{4,12},{8,0},{12,4},{16,24},{20,28},{24,16},{28,20},{1,9},{5... | collective-permute-start | bytes 1572872 | tf_op jit(solution)/shard_map/ppermute | solution.py:226
  226.6 211.2 %collective-permute-start.27 = (f32[128,1536]{1,0:T(8,128)S(1)}, f32[128,1536]{1,0:T(8,128)S(1)}, u32[]{:S(2)}, u32[]{:S(2)}) collective-permute-start(f32[128,1536]{1,0:T(8,128)S(1)} %copy-done.19), channel_id=1, source_target_pairs={{0,4},{4,0},{8,12},{12,8},{16,20},{20,16},{24,28},{28,24},{1,5},{5... | collective-permute-start | bytes 2359304 | tf_op jit(solution)/shard_map/ppermute | solution.py:226
  228.8 142.2 %collective-permute-start.24 = (f32[128,1536]{1,0:T(8,128)S(1)}, f32[128,1536]{1,0:T(8,128)S(1)}, u32[]{:S(2)}, u32[]{:S(2)}) collective-permute-start(f32[128,1536]{1,0:T(8,128)S(1)} %copy-done.22), channel_id=1, source_target_pairs={{0,16},{4,20},{8,24},{12,28},{16,0},{20,4},{24,8},{28,12},{1,17},{... | collective-permute-start | bytes 2359304 | tf_op jit(solution)/shard_map/ppermute | solution.py:226
  229.6 138.4 %collective-permute-start.23 = (f32[128,1536]{1,0:T(8,128)S(1)}, f32[128,1536]{1,0:T(8,128)S(1)}, u32[]{:S(2)}, u32[]{:S(2)}) collective-permute-start(f32[128,1536]{1,0:T(8,128)S(1)} %copy-done.23), channel_id=1, source_target_pairs={{0,20},{4,16},{8,28},{12,24},{16,4},{20,0},{24,12},{28,8},{1,21},{... | collective-permute-start | bytes 2359304 | tf_op jit(solution)/shard_map/ppermute | solution.py:226
  239.0 128.0 %collective-permute-start.22 = (f32[128,1536]{1,0:T(8,128)S(1)}, f32[128,1536]{1,0:T(8,128)S(1)}, u32[]{:S(2)}, u32[]{:S(2)}) collective-permute-start(f32[128,1536]{1,0:T(8,128)S(1)} %copy-done.24), channel_id=1, source_target_pairs={{0,24},{4,28},{8,16},{12,20},{16,8},{20,12},{24,0},{28,4},{1,25},{... | collective-permute-start | bytes 2359304 | tf_op jit(solution)/shard_map/ppermute | solution.py:226
  243.6 58.7 %collective-permute-start.21 = (f32[128,1536]{1,0:T(8,128)S(1)}, f32[128,1536]{1,0:T(8,128)S(1)}, u32[]{:S(2)}, u32[]{:S(2)}) collective-permute-start(f32[128,1536]{1,0:T(8,128)S(1)} %copy-done.25), channel_id=1, source_target_pairs={{0,28},{4,24},{8,20},{12,16},{16,12},{20,8},{24,4},{28,0},{1,29},{... | collective-permute-start | bytes 2359304 | tf_op jit(solution)/shard_map/ppermute | solution.py:226
  302.3 115.8 %collective-permute-start.25 = (f32[128,1536]{1,0:T(8,128)S(1)}, f32[128,1536]{1,0:T(8,128)S(1)}, u32[]{:S(2)}, u32[]{:S(2)}) collective-permute-start(f32[128,1536]{1,0:T(8,128)S(1)} %copy-done.21), channel_id=1, source_target_pairs={{0,12},{4,8},{8,4},{12,0},{16,28},{20,24},{24,20},{28,16},{1,13},{... | collective-permute-start | bytes 2359304 | tf_op jit(solution)/shard_map/ppermute | solution.py:226
  367.0 67.8 %collective-permute-start.26 = (f32[128,1536]{1,0:T(8,128)S(1)}, f32[128,1536]{1,0:T(8,128)S(1)}, u32[]{:S(2)}, u32[]{:S(2)}) collective-permute-start(f32[128,1536]{1,0:T(8,128)S(1)} %copy-done.20), channel_id=1, source_target_pairs={{0,8},{4,12},{8,0},{12,4},{16,24},{20,28},{24,16},{28,20},{1,9},{5... | collective-permute-start | bytes 2359304 | tf_op jit(solution)/shard_map/ppermute | solution.py:226
  368.0 207.6 %collective-permute-start.18 = (f32[128,2048]{1,0:T(8,128)S(1)}, f32[128,2048]{1,0:T(8,128)S(1)}, u32[]{:S(2)}, u32[]{:S(2)}) collective-permute-start(f32[128,2048]{1,0:T(8,128)S(1)} %copy-done.14), channel_id=1, source_target_pairs={{0,12},{4,8},{8,4},{12,0},{16,28},{20,24},{24,20},{28,16},{1,13},{... | collective-permute-start | bytes 3145736 | tf_op jit(solution)/shard_map/ppermute | solution.py:226
  370.9 203.6 %collective-permute-start.17 = (f32[128,2048]{1,0:T(8,128)S(1)}, f32[128,2048]{1,0:T(8,128)S(1)}, u32[]{:S(2)}, u32[]{:S(2)}) collective-permute-start(f32[128,2048]{1,0:T(8,128)S(1)} %copy-done.15), channel_id=1, source_target_pairs={{0,16},{4,20},{8,24},{12,28},{16,0},{20,4},{24,8},{28,12},{1,17},{... | collective-permute-start | bytes 3145736 | tf_op jit(solution)/shard_map/ppermute | solution.py:226
  418.1 153.3 %collective-permute-start.16 = (f32[128,2048]{1,0:T(8,128)S(1)}, f32[128,2048]{1,0:T(8,128)S(1)}, u32[]{:S(2)}, u32[]{:S(2)}) collective-permute-start(f32[128,2048]{1,0:T(8,128)S(1)} %copy-done.16), channel_id=1, source_target_pairs={{0,20},{4,16},{8,28},{12,24},{16,4},{20,0},{24,12},{28,8},{1,21},{... | collective-permute-start | bytes 3145736 | tf_op jit(solution)/shard_map/ppermute | solution.py:226
  434.8 135.5 %collective-permute-start.15 = (f32[128,2048]{1,0:T(8,128)S(1)}, f32[128,2048]{1,0:T(8,128)S(1)}, u32[]{:S(2)}, u32[]{:S(2)}) collective-permute-start(f32[128,2048]{1,0:T(8,128)S(1)} %copy-done.17), channel_id=1, source_target_pairs={{0,24},{4,28},{8,16},{12,20},{16,8},{20,12},{24,0},{28,4},{1,25},{... | collective-permute-start | bytes 3145736 | tf_op jit(solution)/shard_map/ppermute | solution.py:226
  437.8 73.4 %collective-permute-start.14 = (f32[128,2048]{1,0:T(8,128)S(1)}, f32[128,2048]{1,0:T(8,128)S(1)}, u32[]{:S(2)}, u32[]{:S(2)}) collective-permute-start(f32[128,2048]{1,0:T(8,128)S(1)} %copy-done.18), channel_id=1, source_target_pairs={{0,28},{4,24},{8,20},{12,16},{16,12},{20,8},{24,4},{28,0},{1,29},{... | collective-permute-start | bytes 3145736 | tf_op jit(solution)/shard_map/ppermute | solution.py:226
  511.3 86.4 %collective-permute-start.19 = (f32[128,2048]{1,0:T(8,128)S(1)}, f32[128,2048]{1,0:T(8,128)S(1)}, u32[]{:S(2)}, u32[]{:S(2)}) collective-permute-start(f32[128,2048]{1,0:T(8,128)S(1)} %copy-done.13), channel_id=1, source_target_pairs={{0,8},{4,12},{8,0},{12,4},{16,24},{20,28},{24,16},{28,20},{1,9},{5... | collective-permute-start | bytes 3145736 | tf_op jit(solution)/shard_map/ppermute | solution.py:226
  571.4 412.9 %collective-permute-start.78 = (f32[128,1024]{1,0:T(8,128)}, f32[128,1024]{1,0:T(8,128)}, u32[]{:S(2)}, u32[]{:S(2)}) collective-permute-start(f32[128,1024]{1,0:T(8,128)} %get-tuple-element.384), channel_id=1, source_target_pairs={{0,4},{4,0},{8,12},{12,8},{16,20},{20,16},{24,28},{28,24},{1,5},{5... | collective-permute-start | bytes 1572872 | tf_op jit(solution)/shard_map/ppermute | solution.py:226
  574.5 227.3 %collective-permute-start.10 = (f32[128,2560]{1,0:T(8,128)S(1)}, f32[128,2560]{1,0:T(8,128)S(1)}, u32[]{:S(2)}, u32[]{:S(2)}) collective-permute-start(f32[128,2560]{1,0:T(8,128)S(1)} %copy-done.6), channel_id=1, source_target_pairs={{0,16},{4,20},{8,24},{12,28},{16,0},{20,4},{24,8},{28,12},{1,17},{... | collective-permute-start | bytes 3932168 | tf_op jit(solution)/shard_map/ppermute | solution.py:226
  575.6 223.6 %collective-permute-start.9 = (f32[128,2560]{1,0:T(8,128)S(1)}, f32[128,2560]{1,0:T(8,128)S(1)}, u32[]{:S(2)}, u32[]{:S(2)}) collective-permute-start(f32[128,2560]{1,0:T(8,128)S(1)} %copy-done.7), channel_id=1, source_target_pairs={{0,20},{4,16},{8,28},{12,24},{16,4},{20,0},{24,12},{28,8},{1,21},{... | collective-permute-start | bytes 3932168 | tf_op jit(solution)/shard_map/ppermute | solution.py:226
  597.7 198.1 %collective-permute-start.8 = (f32[128,2560]{1,0:T(8,128)S(1)}, f32[128,2560]{1,0:T(8,128)S(1)}, u32[]{:S(2)}, u32[]{:S(2)}) collective-permute-start(f32[128,2560]{1,0:T(8,128)S(1)} %copy-done.8), channel_id=1, source_target_pairs={{0,24},{4,28},{8,16},{12,20},{16,8},{20,12},{24,0},{28,4},{1,25},{... | collective-permute-start | bytes 3932168 | tf_op jit(solution)/shard_map/ppermute | solution.py:226
  599.1 97.5 %collective-permute-start.7 = (f32[128,2560]{1,0:T(8,128)S(1)}, f32[128,2560]{1,0:T(8,128)S(1)}, u32[]{:S(2)}, u32[]{:S(2)}) collective-permute-start(f32[128,2560]{1,0:T(8,128)S(1)} %copy-done.9), channel_id=1, source_target_pairs={{0,28},{4,24},{8,20},{12,16},{16,12},{20,8},{24,4},{28,0},{1,29},{... | collective-permute-start | bytes 3932168 | tf_op jit(solution)/shard_map/ppermute | solution.py:226
  696.6 127.6 %collective-permute-start.11 = (f32[128,2560]{1,0:T(8,128)S(1)}, f32[128,2560]{1,0:T(8,128)S(1)}, u32[]{:S(2)}, u32[]{:S(2)}) collective-permute-start(f32[128,2560]{1,0:T(8,128)S(1)} %copy-done.5), channel_id=1, source_target_pairs={{0,12},{4,8},{8,4},{12,0},{16,28},{20,24},{24,20},{28,16},{1,13},{... | collective-permute-start | bytes 3932168 | tf_op jit(solution)/shard_map/ppermute | solution.py:226
  795.8 48.4 %collective-permute-start.12 = (f32[128,2560]{1,0:T(8,128)S(1)}, f32[128,2560]{1,0:T(8,128)S(1)}, u32[]{:S(2)}, u32[]{:S(2)}) collective-permute-start(f32[128,2560]{1,0:T(8,128)S(1)} %copy-done.4), channel_id=1, source_target_pairs={{0,8},{4,12},{8,0},{12,4},{16,24},{20,28},{24,16},{28,20},{1,9},{5... | collective-permute-start | bytes 3932168 | tf_op jit(solution)/shard_map/ppermute | solution.py:226
  799.2 46.2 %collective-permute-start.13 = (f32[128,2560]{1,0:T(8,128)S(1)}, f32[128,2560]{1,0:T(8,128)S(1)}, u32[]{:S(2)}, u32[]{:S(2)}) collective-permute-start(f32[128,2560]{1,0:T(8,128)S(1)} %get-tuple-element.426), channel_id=1, source_target_pairs={{0,4},{4,0},{8,12},{12,8},{16,20},{20,16},{24,28},{28,24},{1,5},{5... | collective-permute-start | bytes 3932168 | tf_op jit(solution)/shard_map/ppermute | solution.py:226
  884.8 101.7 %collective-permute-start.52 = (f32[128,1280]{1,0:T(8,128)}, f32[128,1280]{1,0:T(8,128)S(1)}, u32[]{:S(2)}, u32[]{:S(2)}) collective-permute-start(f32[128,1280]{1,0:T(8,128)} %constant_dynamic-slice_fusion.58), channel_id=1, source_target_pairs={{0,1},{1,0},{2,3},{3,2},{4,5},{5,4},{6,7},{7,6},{8,9},{9,8},{10,11... | collective-permute-start | bytes 1966088 | tf_op jit(solution)/shard_map/ppermute | solution.py:180
  884.8 158.5 %collective-permute-start.80 = (f32[128,1024]{1,0:T(8,128)S(1)}, f32[128,1024]{1,0:T(8,128)}, u32[]{:S(2)}, u32[]{:S(2)}) collective-permute-start(f32[128,1024]{1,0:T(8,128)S(1)} %copy-done.26), channel_id=1, source_target_pairs={{0,12},{4,8},{8,4},{12,0},{16,28},{20,24},{24,20},{28,16},{1,13},{... | collective-permute-start | bytes 1572872 | tf_op jit(solution)/shard_map/ppermute | solution.py:226
  889.2 150.3 %collective-permute-start.79 = (f32[128,1024]{1,0:T(8,128)}, f32[128,1024]{1,0:T(8,128)}, u32[]{:S(2)}, u32[]{:S(2)}) collective-permute-start(f32[128,1024]{1,0:T(8,128)} %get-tuple-element.394), channel_id=1, source_target_pairs={{0,8},{4,12},{8,0},{12,4},{16,24},{20,28},{24,16},{28,20},{1,9},{5... | collective-permute-start | bytes 1572872 | tf_op jit(solution)/shard_map/ppermute | solution.py:226
  1145.6 55.6 %collective-permute-start.64 = (f32[128,512]{1,0:T(8,128)S(1)}, f32[128,512]{1,0:T(8,128)S(1)}, u32[]{:S(2)}, u32[]{:S(2)}) collective-permute-start(f32[128,512]{1,0:T(8,128)S(1)} %get-tuple-element.175), channel_id=1, source_target_pairs={{0,24},{4,28},{8,16},{12,20},{16,8},{20,12},{24,0},{28,4},{1,25},{... | collective-permute-start | bytes 786440 | tf_op jit(solution)/shard_map/ppermute | solution.py:226
  1177.2 148.7 %collective-permute-start.66 = (f32[128,2560]{1,0:T(8,128)S(1)}, f32[128,2560]{1,0:T(8,128)S(1)}, u32[]{:S(2)}, u32[]{:S(2)}) collective-permute-start(f32[128,2560]{1,0:T(8,128)S(1)} %get-tuple-element.186), channel_id=1, source_target_pairs={{0,16},{4,20},{8,24},{12,28},{16,0},{20,4},{24,8},{28,12},{1,17},{... | collective-permute-start | bytes 3932168 | tf_op jit(solution)/shard_map/ppermute | solution.py:226
  1177.3 255.9 %collective-permute-start.67 = (f32[128,2560]{1,0:T(8,128)S(1)}, f32[128,2560]{1,0:T(8,128)S(1)}, u32[]{:S(2)}, u32[]{:S(2)}) collective-permute-start(f32[128,2560]{1,0:T(8,128)S(1)} %get-tuple-element.187), channel_id=1, source_target_pairs={{0,20},{4,16},{8,28},{12,24},{16,4},{20,0},{24,12},{28,8},{1,21},{... | collective-permute-start | bytes 3932168 | tf_op jit(solution)/shard_map/ppermute | solution.py:226
  1180.5 253.2 %collective-permute-start.68 = (f32[128,2560]{1,0:T(8,128)S(1)}, f32[128,2560]{1,0:T(8,128)S(1)}, u32[]{:S(2)}, u32[]{:S(2)}) collective-permute-start(f32[128,2560]{1,0:T(8,128)S(1)} %get-tuple-element.188), channel_id=1, source_target_pairs={{0,24},{4,28},{8,16},{12,20},{16,8},{20,12},{24,0},{28,4},{1,25},{... | collective-permute-start | bytes 3932168 | tf_op jit(solution)/shard_map/ppermute | solution.py:226
  1182.2 253.6 %collective-permute-start.69 = (f32[128,2560]{1,0:T(8,128)S(1)}, f32[128,2560]{1,0:T(8,128)S(1)}, u32[]{:S(2)}, u32[]{:S(2)}) collective-permute-start(f32[128,2560]{1,0:T(8,128)S(1)} %get-tuple-element.189), channel_id=1, source_target_pairs={{0,28},{4,24},{8,20},{12,16},{16,12},{20,8},{24,4},{28,0},{1,29},{... | collective-permute-start | bytes 3932168 | tf_op jit(solution)/shard_map/ppermute | solution.py:226
  1201.2 96.2 %collective-permute-start.65 = (f32[128,512]{1,0:T(8,128)S(1)}, f32[128,512]{1,0:T(8,128)S(1)}, u32[]{:S(2)}, u32[]{:S(2)}) collective-permute-start(f32[128,512]{1,0:T(8,128)S(1)} %get-tuple-element.176), channel_id=1, source_target_pairs={{0,28},{4,24},{8,20},{12,16},{16,12},{20,8},{24,4},{28,0},{1,29},{... | collective-permute-start | bytes 786440 | tf_op jit(solution)/shard_map/ppermute | solution.py:226
  1297.4 146.4 %collective-permute-start.70 = (f32[128,1024]{1,0:T(8,128)S(1)}, f32[128,1024]{1,0:T(8,128)S(1)}, u32[]{:S(2)}, u32[]{:S(2)}) collective-permute-start(f32[128,1024]{1,0:T(8,128)S(1)} %get-tuple-element.201), channel_id=1, source_target_pairs={{0,4},{4,0},{8,12},{12,8},{16,20},{20,16},{24,28},{28,24},{1,5},{5... | collective-permute-start | bytes 1572872 | tf_op jit(solution)/shard_map/ppermute | solution.py:226
  1326.0 141.3 %collective-permute-start.71 = (f32[128,1024]{1,0:T(8,128)S(1)}, f32[128,1024]{1,0:T(8,128)S(1)}, u32[]{:S(2)}, u32[]{:S(2)}) collective-permute-start(f32[128,1024]{1,0:T(8,128)S(1)} %get-tuple-element.202), channel_id=1, source_target_pairs={{0,8},{4,12},{8,0},{12,4},{16,24},{20,28},{24,16},{28,20},{1,9},{5... | collective-permute-start | bytes 1572872 | tf_op jit(solution)/shard_map/ppermute | solution.py:226
  1433.3 44.3 %collective-permute-start.72 = (f32[128,1024]{1,0:T(8,128)S(1)}, f32[128,1024]{1,0:T(8,128)S(1)}, u32[]{:S(2)}, u32[]{:S(2)}) collective-permute-start(f32[128,1024]{1,0:T(8,128)S(1)} %get-tuple-element.203), channel_id=1, source_target_pairs={{0,12},{4,8},{8,4},{12,0},{16,28},{20,24},{24,20},{28,16},{1,13},{... | collective-permute-start | bytes 1572872 | tf_op jit(solution)/shard_map/ppermute | solution.py:226
  1433.7 116.8 %collective-permute-start.73 = (f32[128,2048]{1,0:T(8,128)S(1)}, f32[128,2048]{1,0:T(8,128)S(1)}, u32[]{:S(2)}, u32[]{:S(2)}) collective-permute-start(f32[128,2048]{1,0:T(8,128)S(1)} %get-tuple-element.214), channel_id=1, source_target_pairs={{0,16},{4,20},{8,24},{12,28},{16,0},{20,4},{24,8},{28,12},{1,17},{... | collective-permute-start | bytes 3145736 | tf_op jit(solution)/shard_map/ppermute | solution.py:226
  1435.9 137.7 %collective-permute-start.74 = (f32[128,2048]{1,0:T(8,128)S(1)}, f32[128,2048]{1,0:T(8,128)S(1)}, u32[]{:S(2)}, u32[]{:S(2)}) collective-permute-start(f32[128,2048]{1,0:T(8,128)S(1)} %get-tuple-element.215), channel_id=1, source_target_pairs={{0,20},{4,16},{8,28},{12,24},{16,4},{20,0},{24,12},{28,8},{1,21},{... | collective-permute-start | bytes 3145736 | tf_op jit(solution)/shard_map/ppermute | solution.py:226
  1443.8 129.8 %collective-permute-start.75 = (f32[128,2048]{1,0:T(8,128)S(1)}, f32[128,2048]{1,0:T(8,128)S(1)}, u32[]{:S(2)}, u32[]{:S(2)}) collective-permute-start(f32[128,2048]{1,0:T(8,128)S(1)} %get-tuple-element.216), channel_id=1, source_target_pairs={{0,24},{4,28},{8,16},{12,20},{16,8},{20,12},{24,0},{28,4},{1,25},{... | collective-permute-start | bytes 3145736 | tf_op jit(solution)/shard_map/ppermute | solution.py:226
  1467.3 106.3 %collective-permute-start.76 = (f32[128,2048]{1,0:T(8,128)S(1)}, f32[128,2048]{1,0:T(8,128)S(1)}, u32[]{:S(2)}, u32[]{:S(2)}) collective-permute-start(f32[128,2048]{1,0:T(8,128)S(1)} %get-tuple-element.217), channel_id=1, source_target_pairs={{0,28},{4,24},{8,20},{12,16},{16,12},{20,8},{24,4},{28,0},{1,29},{... | collective-permute-start | bytes 3145736 | tf_op jit(solution)/shard_map/ppermute | solution.py:226
  1477.6 112.8 %collective-permute-start.77 = (f32[512,1024]{1,0:T(8,128)S(1)}, f32[512,1024]{1,0:T(8,128)S(1)}, u32[]{:S(2)}, u32[]{:S(2)}) collective-permute-start(f32[512,1024]{1,0:T(8,128)S(1)} %slice.161), channel_id=1, source_target_pairs={{0,16},{4,20},{8,24},{12,28},{1,17},{5,21},{9,25},{13,29},{2,18},{... | collective-permute-start | bytes 6291464 | tf_op jit(solution)/shard_map/ppermute | solution.py:253
  1621.8 170.8 %collective-permute-start.81 = (f32[128,1024]{1,0:T(8,128)S(1)}, f32[128,1024]{1,0:T(8,128)S(1)}, u32[]{:S(2)}, u32[]{:S(2)}) collective-permute-start(f32[128,1024]{1,0:T(8,128)S(1)} %get-tuple-element.230), channel_id=1, source_target_pairs={{0,4},{4,0},{8,12},{12,8},{16,20},{20,16},{24,28},{28,24},{1,5},{5... | collective-permute-start | bytes 1572872 | tf_op jit(solution)/shard_map/ppermute | solution.py:226
  1622.8 175.3 %collective-permute-start.82 = (f32[128,1024]{1,0:T(8,128)S(1)}, f32[128,1024]{1,0:T(8,128)S(1)}, u32[]{:S(2)}, u32[]{:S(2)}) collective-permute-start(f32[128,1024]{1,0:T(8,128)S(1)} %get-tuple-element.231), channel_id=1, source_target_pairs={{0,8},{4,12},{8,0},{12,4},{16,24},{20,28},{24,16},{28,20},{1,9},{5... | collective-permute-start | bytes 1572872 | tf_op jit(solution)/shard_map/ppermute | solution.py:226
  1737.9 61.6 %collective-permute-start.83 = (f32[128,1024]{1,0:T(8,128)S(1)}, f32[128,1024]{1,0:T(8,128)S(1)}, u32[]{:S(2)}, u32[]{:S(2)}) collective-permute-start(f32[128,1024]{1,0:T(8,128)S(1)} %get-tuple-element.232), channel_id=1, source_target_pairs={{0,12},{4,8},{8,4},{12,0},{16,28},{20,24},{24,20},{28,16},{1,13},{... | collective-permute-start | bytes 1572872 | tf_op jit(solution)/shard_map/ppermute | solution.py:226
  1738.1 68.2 %collective-permute-start.84 = (f32[128,2560]{1,0:T(8,128)S(1)}, f32[128,2560]{1,0:T(8,128)S(1)}, u32[]{:S(2)}, u32[]{:S(2)}) collective-permute-start(f32[128,2560]{1,0:T(8,128)S(1)} %get-tuple-element.244), channel_id=1, source_target_pairs={{0,4},{4,0},{8,12},{12,8},{16,20},{20,16},{24,28},{28,24},{1,5},{5... | collective-permute-start | bytes 3932168 | tf_op jit(solution)/shard_map/ppermute | solution.py:226
  1739.3 68.4 %collective-permute-start.85 = (f32[128,2560]{1,0:T(8,128)S(1)}, f32[128,2560]{1,0:T(8,128)S(1)}, u32[]{:S(2)}, u32[]{:S(2)}) collective-permute-start(f32[128,2560]{1,0:T(8,128)S(1)} %get-tuple-element.245), channel_id=1, source_target_pairs={{0,8},{4,12},{8,0},{12,4},{16,24},{20,28},{24,16},{28,20},{1,9},{5... | collective-permute-start | bytes 3932168 | tf_op jit(solution)/shard_map/ppermute | solution.py:226
  1792.6 51.6 %collective-permute-start.86 = (f32[128,2560]{1,0:T(8,128)S(1)}, f32[128,2560]{1,0:T(8,128)S(1)}, u32[]{:S(2)}, u32[]{:S(2)}) collective-permute-start(f32[128,2560]{1,0:T(8,128)S(1)} %get-tuple-element.246), channel_id=1, source_target_pairs={{0,12},{4,8},{8,4},{12,0},{16,28},{20,24},{24,20},{28,16},{1,13},{... | collective-permute-start | bytes 3932168 | tf_op jit(solution)/shard_map/ppermute | solution.py:226
  1798.1 210.1 %collective-permute-start.97 = (f32[128,512]{1,0:T(8,128)S(1)}, f32[128,512]{1,0:T(8,128)S(1)}, u32[]{:S(2)}, u32[]{:S(2)}) collective-permute-start(f32[128,512]{1,0:T(8,128)S(1)} %get-tuple-element.300), channel_id=1, source_target_pairs={{0,4},{4,0},{8,12},{12,8},{16,20},{20,16},{24,28},{28,24},{1,5},{5... | collective-permute-start | bytes 786440 | tf_op jit(solution)/shard_map/ppermute | solution.py:226
  1799.4 50.3 %collective-permute-start.87 = (f32[128,1536]{1,0:T(8,128)S(1)}, f32[128,1536]{1,0:T(8,128)S(1)}, u32[]{:S(2)}, u32[]{:S(2)}) collective-permute-start(f32[128,1536]{1,0:T(8,128)S(1)} %get-tuple-element.257), channel_id=1, source_target_pairs={{0,16},{4,20},{8,24},{12,28},{16,0},{20,4},{24,8},{28,12},{1,17},{... | collective-permute-start | bytes 2359304 | tf_op jit(solution)/shard_map/ppermute | solution.py:226
  1806.3 99.0 %collective-permute-start.88 = (f32[128,1536]{1,0:T(8,128)S(1)}, f32[128,1536]{1,0:T(8,128)S(1)}, u32[]{:S(2)}, u32[]{:S(2)}) collective-permute-start(f32[128,1536]{1,0:T(8,128)S(1)} %get-tuple-element.258), channel_id=1, source_target_pairs={{0,20},{4,16},{8,28},{12,24},{16,4},{20,0},{24,12},{28,8},{1,21},{... | collective-permute-start | bytes 2359304 | tf_op jit(solution)/shard_map/ppermute | solution.py:226
  1807.7 98.8 %collective-permute-start.89 = (f32[128,1536]{1,0:T(8,128)S(1)}, f32[128,1536]{1,0:T(8,128)S(1)}, u32[]{:S(2)}, u32[]{:S(2)}) collective-permute-start(f32[128,1536]{1,0:T(8,128)S(1)} %get-tuple-element.259), channel_id=1, source_target_pairs={{0,24},{4,28},{8,16},{12,20},{16,8},{20,12},{24,0},{28,4},{1,25},{... | collective-permute-start | bytes 2359304 | tf_op jit(solution)/shard_map/ppermute | solution.py:226
  1844.2 78.2 %collective-permute-start.90 = (f32[128,1536]{1,0:T(8,128)S(1)}, f32[128,1536]{1,0:T(8,128)S(1)}, u32[]{:S(2)}, u32[]{:S(2)}) collective-permute-start(f32[128,1536]{1,0:T(8,128)S(1)} %get-tuple-element.260), channel_id=1, source_target_pairs={{0,28},{4,24},{8,20},{12,16},{16,12},{20,8},{24,4},{28,0},{1,29},{... | collective-permute-start | bytes 2359304 | tf_op jit(solution)/shard_map/ppermute | solution.py:226
  1849.7 160.3 %collective-permute-start.98 = (f32[128,512]{1,0:T(8,128)S(1)}, f32[128,512]{1,0:T(8,128)S(1)}, u32[]{:S(2)}, u32[]{:S(2)}) collective-permute-start(f32[128,512]{1,0:T(8,128)S(1)} %get-tuple-element.301), channel_id=1, source_target_pairs={{0,8},{4,12},{8,0},{12,4},{16,24},{20,28},{24,16},{28,20},{1,9},{5... | collective-permute-start | bytes 786440 | tf_op jit(solution)/shard_map/ppermute | solution.py:226
  1922.5 43.2 %collective-permute-start.93 = (f32[128,2048]{1,0:T(8,128)S(1)}, f32[128,2048]{1,0:T(8,128)S(1)}, u32[]{:S(2)}, u32[]{:S(2)}) collective-permute-start(f32[128,2048]{1,0:T(8,128)S(1)} %get-tuple-element.274), channel_id=1, source_target_pairs={{0,12},{4,8},{8,4},{12,0},{16,28},{20,24},{24,20},{28,16},{1,13},{... | collective-permute-start | bytes 3145736 | tf_op jit(solution)/shard_map/ppermute | solution.py:226
  1982.7 56.8 %collective-permute-start.104 = (f32[128,512]{1,0:T(8,128)S(1)}, f32[128,512]{1,0:T(8,128)S(1)}, u32[]{:S(2)}, u32[]{:S(2)}) collective-permute-start(f32[128,512]{1,0:T(8,128)S(1)} %get-tuple-element.324), channel_id=1, source_target_pairs={{0,4},{4,0},{8,12},{12,8},{16,20},{20,16},{24,28},{28,24},{1,5},{5... | collective-permute-start | bytes 786440 | tf_op jit(solution)/shard_map/ppermute | solution.py:226
  (85 other events, 3190.6 us)
